TPU v7x, 256 devices: a whole 4x4x8 slice. The times are simulated.
256 devices in a mesh: state: 8 (over z), act: 32 (over x, y, core).
Axes of the slice: x: 4, y: 4, z: 8, core: 2. Of those that a mesh axis runs over, the one named last changes fastest.
Arguments:
- state_features: bfloat16 [768, 2048], P('state', 'act'), may hold values from -6 to 6
- action_features: bfloat16 [768, 256, 2048], P('state', 'act'), may hold values from -240 to 240
- targets: float32 [768], P('state'), may hold values from -12 to 12
- w_hidden: bfloat16 [2048, 2048], replicated, may hold values from -0.125 to 0.125
- w_head: float32 [2048], replicated, may hold values from -7 to 7
Outputs:
- grad_hidden: float32 [2048, 2048], P(('state', 'act'))
- grad_head: float32 [2048], replicated
- log_partition: float32 [768], P('state')
- mean_loss: float32 [], replicated
All inputs are finite; a program needn't handle non-finite values.
Results may differ from a plain program's by a relative error of at most 0.006.
Values may be sent and summed in bfloat16 or wider, within the bound.
No kernel may reach another device: no remote copies, remote signals or barrier semaphores. Data moves between devices by JAX's collectives and lax.ppermute only.
A program may use at most 128 MiB of HBM per device.

v0:
```python
import functools

import jax
import jax.numpy as jnp
from jax import lax
from jax.sharding import Mesh
from jax.sharding import PartitionSpec as P

ACT = ("act_0", "act_1", "act_2")
STATE_ACT = ("state", "act_0", "act_1", "act_2")


norm_epsilon = 1e-06
penalty_weight = 2.0


def sent_to_all(value, axis):
    copies = jnp.broadcast_to(value, (lax.axis_size(axis), *value.shape))
    return lax.all_to_all(copies, axis, split_axis=0, concat_axis=0, tiled=True)


def joined_along(parts, dim):
    parts = jnp.moveaxis(parts, 0, dim)
    dims = parts.shape
    return parts.reshape(*dims[:dim], dims[dim] * dims[dim + 1], *dims[dim + 2 :])


def collect(value, axis, dim):
    parts = sent_to_all(value, axis)
    return joined_along(parts, dim)


def taken_together(value, axis):
    everything = sent_to_all(value, axis)
    return jnp.max(everything, axis=0)


def of_everyone(value, axis):
    everything = sent_to_all(value, axis)
    return jnp.sum(everything, axis=0)


def split_up(value, dim, count):
    dims = value.shape
    parts = value.reshape(*dims[:dim], count, dims[dim] // count, *dims[dim + 1 :])
    return jnp.moveaxis(parts, dim, 0)


def sum_at_owner(value, axis, dim):
    count = lax.axis_size(axis)
    parts = lax.all_to_all(split_up(value, dim, count), axis, 0, 0, tiled=True)
    return jnp.sum(parts, axis=0)


def over_axes(value, axes):
    return functools.reduce(lax.psum, axes, value)


def body(state_features, action_features, targets, w_hidden, w_head):
    states_here, actions_here, width = action_features.shape
    state_count = lax.axis_size("state")
    states_total = states_here * state_count
    whole_states = collect(state_features, ACT, 1)
    mixture = whole_states.astype(jnp.float32)[:, None, :] + action_features.astype(jnp.float32)
    normed = (
        mixture * lax.rsqrt(jnp.mean(mixture * mixture, -1, keepdims=True) + norm_epsilon)
    ).astype(jnp.bfloat16)
    flat_rows = normed.reshape(-1, width)
    preact = jnp.dot(flat_rows, w_hidden, preferred_element_type=jnp.float32)
    sigmoid_pre = jax.nn.sigmoid(preact)
    head_input = flat_rows.astype(jnp.float32) + preact * sigmoid_pre
    scores = jnp.sum(head_input * w_head, -1).reshape(states_here, actions_here)
    row_max = jnp.max(scores, -1)
    global_max = taken_together(row_max, ACT)
    local_sum = jnp.sum(jnp.exp(scores - global_max[:, None]), -1)
    log_partition = global_max + jnp.log(of_everyone(local_sum, ACT))
    softmax_weight = jnp.exp(scores - log_partition[:, None])
    action_index = lax.axis_index(ACT) * actions_here + jnp.arange(actions_here, dtype=jnp.int32)
    is_data = (action_index == 0)[None, :]
    bellman_gap = scores - targets[:, None]
    score_grad = penalty_weight * softmax_weight + jnp.where(
        is_data, bellman_gap - penalty_weight, 0.0
    )
    loss_terms = jnp.where(
        is_data,
        penalty_weight * (log_partition[:, None] - scores) + 0.5 * bellman_gap * bellman_gap,
        0.0,
    )
    grad_flat = score_grad.reshape(-1)
    head_local = jnp.sum(grad_flat[:, None] * head_input, 0)
    back_grad = (
        grad_flat[:, None] * w_head * (sigmoid_pre + preact * sigmoid_pre * (1.0 - sigmoid_pre))
    ).astype(jnp.bfloat16)
    grad_slab = lax.psum_scatter(
        lax.dot_general(
            flat_rows, back_grad, (((0,), (0,)), ((), ())), preferred_element_type=jnp.float32
        ),
        "state",
        scatter_dimension=0,
        tiled=True,
    )
    grad_hidden = sum_at_owner(grad_slab, ACT, 0)
    grad_head, loss_sum = (
        over_axes(head_local, STATE_ACT),
        over_axes(jnp.sum(loss_terms), STATE_ACT),
    )
    return (grad_hidden, grad_head, log_partition, loss_sum / states_total)


def solution(mesh):
    finer = Mesh(
        mesh.devices.reshape(mesh.shape["state"], 4, 4, 2), ("state", "act_0", "act_1", "act_2")
    )
    placed = (P("state", ACT), P("state", ACT, None), P("state"), P(), P())
    return jax.shard_map(
        body,
        mesh=finer,
        in_specs=placed,
        out_specs=(P(STATE_ACT, None), P(), P("state"), P()),
        check_vma=False,
    )
```

profile of v0, /device:TPU:1, one launch (start us, length us, event | category | flops | bytes accessed | tf_op | source)
XLA Modules:
  0.0 324.3 jit_solution(5015506502604255950)
XLA Ops:
  7.2 0.0 copy-start
  7.2 0.0 copy-start.3
  7.2 1.0 broadcast_in_dim.38
  8.2 20.0 %all_to_all.22 = bf16[32,96,64]{1,2,0:T(8,128)(2,1)S(1)} all-to-all(bf16[32,96,64]{1,2,0:T(8,128)(2,1)S(1)} %broadcast_in_dim.38), channel_id=1, replica_groups=mesh['state'=8,'act_0'=4,'act_1'=4,'act_2'=2] {'act_0','act_1','act_2'}, dimensions={0} | all-to-all | bytes 786432 | tf_op jit(solution)/shard_map/all_to_all | solution.py:19
  28.1 1.1 convert_element_type.33
  29.2 2.5 copy.19
  31.7 0.0 copy-done
  31.7 2.0 multiply_reduce_fusion.2
  33.8 0.1 copy.20
  33.8 0.1 copy.21
  33.9 0.0 copy-done.3
  33.9 0.0 copy-start.1
  34.0 13.4 %multiply_reduce_fusion.1 = (f32[768]{0:T(1024)S(1)}, f32[768,2048]{1,0:T(8,128)}) fusion(f32[2048]{0:T(1024)S(1)} %copy-done.3, f32[96,8]{1,0:T(8,128)S(1)} %copy.21, bf16[96,8,2048]{2,1,0:T(8,128)(2,1)S(1)} %copy-done, f32[96,2048]{1,0:T(8,128)} %copy.19, bf16[2048,2048]{1,0:T(8,128)(2,1)} %param.8), kind=kOutput, calls=%fused_computation.2 | convolution fusion | flops 6467615744 | bytes 18626560 | tf_op jit(solution)/shard_map/dot_general | solution.py:69
  47.3 0.1 reshape.91
  47.4 0.1 reduce_max.18
  47.5 0.6 broadcast_in_dim.39
  48.2 3.6 %all-to-all-start.1 = ((f32[32,1,96]{2,1,0:T(1,128)}), f32[32,1,96]{2,1,0:T(1,128)S(1)}, u32[]{:S(2)}, u32[]{:S(2)}) async-start(f32[32,1,96]{2,1,0:T(1,128)} %broadcast_in_dim.39), calls=%async_computation.1 | async-start | bytes 32768 | tf_op jit(solution)/shard_map/all_to_all | solution.py:19
  51.8 6.9 %all-to-all-done.1 = f32[32,1,96]{2,1,0:T(1,128)S(1)} async-done(((f32[32,1,96]{2,1,0:T(1,128)}), f32[32,1,96]{2,1,0:T(1,128)S(1)}, u32[]{:S(2)}, u32[]{:S(2)}) %all-to-all-start.1) | async-done | bytes 12320 | tf_op jit(solution)/shard_map/all_to_all | solution.py:19
  58.7 0.2 exponential_reduce_fusion
  58.9 0.6 broadcast_in_dim.40
  59.5 4.1 %all-to-all-start.2 = ((f32[32,1,96]{2,1,0:T(1,128)}), f32[32,1,96]{2,1,0:T(1,128)S(1)}, u32[]{:S(2)}, u32[]{:S(2)}) async-start(f32[32,1,96]{2,1,0:T(1,128)} %broadcast_in_dim.40), calls=%async_computation.2 | async-start | bytes 32768 | tf_op jit(solution)/shard_map/all_to_all | solution.py:19
  63.7 0.0 reduce-scatter.2.cloned.1.call-start
  63.7 0.1 broadcast_in_dim.42
  63.8 0.0 copy-done.1
  63.9 0.1 sub.63
  63.9 0.1 sub.64
  64.0 6.6 %all-to-all-done.2 = f32[32,1,96]{2,1,0:T(1,128)S(1)} async-done(((f32[32,1,96]{2,1,0:T(1,128)}), f32[32,1,96]{2,1,0:T(1,128)S(1)}, u32[]{:S(2)}, u32[]{:S(2)}) %all-to-all-start.2) | async-done | bytes 12320 | tf_op jit(solution)/shard_map/all_to_all | solution.py:19
  70.7 0.0 copy-start.2
  70.7 0.1 sub.60
  70.8 0.1 sub.61
  70.9 14.0 %fusion.2 = f32[2048,2048]{1,0:T(8,128)} fusion(f32[768,2048]{1,0:T(8,128)} %get-tuple-element.13, f32[768]{0:T(1024)S(1)} %select_add_fusion, f32[2048]{0:T(1024)S(1)} %copy-done.3, bf16[96,8,2048]{2,1,0:T(8,128)(2,1)S(1)} %copy-done, f32[96,8]{1,0:T(8,128)S(1)} %copy.21, f32[96,2048]{1,0:T(8,128)} %copy.19), kind=kOutput, calls=%fused_computation.10 | convolution fusion | flops 6464471040 | bytes 27015168 | tf_op jit(solution)/shard_map/dot_general | solution.py:95
  84.9 0.0 reduce-scatter.2.cloned.1.call-update
  84.9 172.8 %reduce-scatter.2.cloned.1.call-done = f32[256,2048]{1,0:T(8,128)} async-done(((f32[2048,2048]{1,0:T(8,128)}), f32[256,2048]{1,0:T(8,128)}) %reduce-scatter.2.cloned.1.call-update) | async-done | bytes 2097168 | tf_op jit(solution)/shard_map/reduce_scatter | solution.py:94
  257.7 7.6 %all-to-all-start.3 = ((f32[32,8,2048]{2,1,0:T(8,128)}), f32[32,8,2048]{2,1,0:T(8,128)}, u32[]{:S(2)}, u32[]{:S(2)}) async-start(f32[32,8,2048]{2,1,0:T(8,128)} %bitcast.18), calls=%async_computation.4 | async-start | bytes 4194304 | tf_op jit(solution)/shard_map/all_to_all | solution.py:51
  265.4 0.0 copy-done.2
  265.4 0.7 fusion.8
  266.1 4.6 %multiply_reduce_fusion = f32[2048]{0:T(1024)S(1)} fusion(f32[768]{0:T(1024)S(1)} %select_add_fusion, f32[96,8]{1,0:T(8,128)S(1)} %copy.21, bf16[96,8,2048]{2,1,0:T(8,128)(2,1)S(1)} %copy-done, f32[96,2048]{1,0:T(8,128)} %copy.19, f32[768,2048]{1,0:T(8,128)} %get-tuple-element.13), kind=kLoop, calls=%fused_computation | loop fusion | flops 18872320 | bytes 10237952 | tf_op jit(solution)/shard_map/reduce_sum | solution.py:90
  270.7 14.5 %all-reduce = (f32[2048]{0:T(1024)S(1)}, f32[]{:T(128)}) all-reduce(f32[2048]{0:T(1024)S(1)} %multiply_reduce_fusion, f32[]{:T(128)} %fusion.8), channel_id=1, replica_groups=mesh['state'=8,'act_0'=4,'act_1'=4,'act_2'=2] {'state'}, use_global_device_ids=true, to_apply=%region_9.10 | all-reduce | flops 2049 | bytes 16392 | tf_op jit(solution)/shard_map/psum | solution.py:56
  285.2 10.1 %all-reduce.2 = (f32[2048]{0:T(1024)S(1)}, f32[]{:T(128)}) all-reduce(f32[2048]{0:T(1024)S(1)} %get-tuple-element.4, f32[]{:T(128)} %get-tuple-element.5), channel_id=1, replica_groups=mesh['state'=8,'act_0'=4,'act_1'=4,'act_2'=2] {'act_0'}, use_global_device_ids=true, to_apply=%region_10.11 | all-reduce | flops 2049 | bytes 16392 | tf_op jit(solution)/shard_map/psum | solution.py:56
  295.3 9.0 %all-reduce.1 = (f32[2048]{0:T(1024)S(1)}, f32[]{:T(128)}) all-reduce(f32[2048]{0:T(1024)S(1)} %get-tuple-element.8, f32[]{:T(128)} %get-tuple-element.9), channel_id=1, replica_groups=mesh['state'=8,'act_0'=4,'act_1'=4,'act_2'=2] {'act_1'}, use_global_device_ids=true, to_apply=%region_11.12 | all-reduce | flops 2049 | bytes 16392 | tf_op jit(solution)/shard_map/psum | solution.py:56
  304.3 9.0 %all-reduce.3 = (f32[2048]{0:T(1024)}, f32[]{:T(128)}) all-reduce(f32[2048]{0:T(1024)S(1)} %get-tuple-element.6, f32[]{:T(128)} %get-tuple-element.7), channel_id=1, replica_groups=mesh['state'=8,'act_0'=4,'act_1'=4,'act_2'=2] {'act_2'}, use_global_device_ids=true, to_apply=%region_12.13 | all-reduce | flops 2049 | bytes 16392 | tf_op jit(solution)/shard_map/psum | solution.py:56
  314.0 0.0 all-to-all-done.3
  314.0 2.3 reduce_sum.67
  (7 shorter events, 0.1 us)
Async XLA Ops:
  7.2 24.6 %copy-start = (bf16[96,8,2048]{2,1,0:T(8,128)(2,1)S(1)}, bf16[96,8,2048]{2,1,0:T(8,128)(2,1)}, u32[]{:S(2)}) copy-start(bf16[96,8,2048]{2,1,0:T(8,128)(2,1)} %param.6) | copy-start | bytes 9437188
  7.2 26.8 %copy-start.3 = (f32[2048]{0:T(1024)S(1)}, f32[2048]{0:T(1024)}, u32[]{:S(2)}) copy-start(f32[2048]{0:T(1024)} %param.9) | copy-start | bytes 24580
  33.9 29.9 %copy-start.1 = (f32[96]{0:T(128)S(1)}, f32[96]{0:T(128)}, u32[]{:S(2)}) copy-start(f32[96]{0:T(128)} %param.7) | copy-start | bytes 1156
  48.2 10.5 %all-to-all-start.1 = ((f32[32,1,96]{2,1,0:T(1,128)}), f32[32,1,96]{2,1,0:T(1,128)S(1)}, u32[]{:S(2)}, u32[]{:S(2)}) async-start(f32[32,1,96]{2,1,0:T(1,128)} %broadcast_in_dim.39), calls=%async_computation.1 | async-start | bytes 32768 | tf_op jit(solution)/shard_map/all_to_all | solution.py:19
  59.5 11.2 %all-to-all-start.2 = ((f32[32,1,96]{2,1,0:T(1,128)}), f32[32,1,96]{2,1,0:T(1,128)S(1)}, u32[]{:S(2)}, u32[]{:S(2)}) async-start(f32[32,1,96]{2,1,0:T(1,128)} %broadcast_in_dim.40), calls=%async_computation.2 | async-start | bytes 32768 | tf_op jit(solution)/shard_map/all_to_all | solution.py:19
  63.7 194.1 %reduce-scatter.2.cloned.1.call-start = ((), (), s32[]{:S(2)}) async-start(), calls=%async_computation.5 | async-start | bytes 18874368 | tf_op jit(solution)/shard_map/reduce_scatter | solution.py:94
  70.7 194.7 %copy-start.2 = (f32[96]{0:T(128)}, f32[96]{0:T(128)S(1)}, u32[]{:S(2)}) copy-start(f32[96]{0:T(128)S(1)} %log_add_fusion) | copy-start | bytes 1156
  257.7 56.2 %all-to-all-start.3 = ((f32[32,8,2048]{2,1,0:T(8,128)}), f32[32,8,2048]{2,1,0:T(8,128)}, u32[]{:S(2)}, u32[]{:S(2)}) async-start(f32[32,8,2048]{2,1,0:T(8,128)} %bitcast.18), calls=%async_computation.4 | async-start | bytes 4194304 | tf_op jit(solution)/shard_map/all_to_all | solution.py:51
Sparse Core Ops, SparseCore 0:
  85.1 172.6 reduce-scatter.1
where the time goes:
time: 325 us; the launch traced here: 324 us
  waiting for transfers between devices  186 us (57%)
  blocking collectives  62.6 us (19%)
  matrix products  27.4 us (8%)
  between operations  16 us (5%)
  starting transfers between devices  15.4 us (5%)
  other arithmetic  11.1 us (3%)
  local copies, waits for them, and re-layouts  5.41 us (2%)
    reduce_scatter x1, waiting for transfers between devices, body(): lax.psum_scatter(lax.dot_general(flat_rows, back_grad, (((0,), (0,)), (()...  173 us
    psum x4, blocking collectives, over_axes(): return functools.reduce(lax.psum, axes, value)  42.7 us
    all_to_all x1, blocking collectives, sent_to_all(): return lax.all_to_all(copies, axis, split_axis=0, concat_axis=0, tiled=True)  20 us
    dot_general x1, matrix products, body(): lax.dot_general(flat_rows, back_grad, (((0,), (0,)), ((), ())), preferred...  14 us
    all_to_all x2, waiting for transfers between devices, sent_to_all(): return lax.all_to_all(copies, axis, split_axis=0, concat_axis=0, tiled=True)  13.5 us
    dot_general x1, matrix products, body(): preact = jnp.dot(flat_rows, w_hidden, preferred_element_type=jnp.float32)  13.4 us
    all_to_all x2, starting transfers between devices, sent_to_all(): return lax.all_to_all(copies, axis, split_axis=0, concat_axis=0, tiled=True)  7.76 us
    all_to_all x1, starting transfers between devices, sum_at_owner(): parts = lax.all_to_all(split_up(value, dim, count), axis, 0, 0, tiled=True)  7.64 us
  transfers between devices with their start and end apart: 4, of which 3 were waited for; matrix products, arithmetic and copies ran while one was open for 2% of the time, Pallas kernels for 0%

commit v1 on v0

v1 whole, which is shorter than its diff:
```python
import functools

import jax
import jax.numpy as jnp
from jax import lax
from jax.experimental import pallas as pl
from jax.experimental.pallas import tpu as pltpu
from jax.sharding import Mesh
from jax.sharding import PartitionSpec as P

ACT = ("x", "y", "c")
EVERY = ("z", "x", "y", "c")
F32 = jnp.float32
BF16 = jnp.bfloat16

norm_epsilon = 1e-06
penalty_weight = 2.0


ROWS = 256
COLS = 256


def shifted(value, axis, step):
    count = lax.axis_size(axis)
    return lax.ppermute(value, axis, [(i, (i + step) % count) for i in range(count)])


def within(value, op):
    lane = lax.broadcasted_iota(jnp.int32, value.shape, 1)
    width = value.shape[1]
    for step in (1, 2, 4):
        low = pltpu.roll(value, step, 1)
        high = pltpu.roll(value, width - step, 1)
        value = op(value, jnp.where((lane & step) != 0, low, high))
    return value


def forward_kernel(core_ref, s_ref, a_ref, w_ref, head_ref, xt_ref, keep_ref, send_ref, h_ref, score_ref, stats_ref, x_ref, tally_ref):
    height, width = a_ref.shape
    tiles = width // COLS
    at = pl.program_id(0)

    def normalise(i, carry):
        row = pl.multiple_of(i * 16, 16)
        acts = a_ref[pl.ds(row, 16), :].astype(F32)
        first = jnp.broadcast_to(s_ref[pl.ds(2 * i, 1), :], (8, width))
        second = jnp.broadcast_to(s_ref[pl.ds(2 * i + 1, 1), :], (8, width))
        mixture = jnp.concatenate([first, second], 0) + acts
        scale = lax.rsqrt(jnp.mean(mixture * mixture, -1, keepdims=True) + norm_epsilon)
        x_ref[pl.ds(row, 16), :] = (mixture * scale).astype(BF16)
        return carry

    lax.fori_loop(0, height // 16, normalise, 0)
    core = core_ref[0]
    total = jnp.zeros((height, 128), F32)
    x = x_ref[...]
    for j in range(tiles):
        n = pl.multiple_of(lax.rem(j + core * (tiles // 2), tiles) * COLS, COLS)
        x_cols = x_ref[:, pl.ds(n, COLS)]
        xt_ref[pl.ds(n, COLS), :] = x_cols.T
        preact = jnp.dot(x, w_ref[:, pl.ds(n, COLS)], preferred_element_type=F32)
        g = jax.nn.sigmoid(preact)
        gated = preact * g
        h = x_cols.astype(F32) + gated
        head = head_ref[:, pl.ds(n, COLS)]
        h_ref[:, pl.ds(n, COLS)] = h.astype(BF16)
        u = (head * (g + gated * (1.0 - g))).astype(BF16)
        if j < tiles // 2:
            keep_ref[:, j * COLS : (j + 1) * COLS] = u
        else:
            send_ref[:, j * COLS - width // 2 : (j + 1) * COLS - width // 2] = u
        part = h * head
        for k in range(COLS // 128):
            total += part[:, k * 128 : (k + 1) * 128]
    score = jnp.sum(total.T, 0, keepdims=True)
    score_ref[...] = score
    score = jnp.broadcast_to(score, (8, height))
    peak = within(score, jnp.maximum)
    mass = within(jnp.exp(score - peak), jnp.add)
    pair = jnp.where(lax.broadcasted_iota(jnp.int32, score.shape, 0) == 0, peak, mass)
    row = lax.broadcasted_iota(jnp.int32, (height, 128), 0)
    lane = lax.broadcasted_iota(jnp.int32, (height, 128), 1)
    pick = (row == (lane - at * (height // 8)) * 8).astype(F32)
    packed = jnp.dot(pair, pick, precision=lax.Precision.HIGHEST, preferred_element_type=F32)

    @pl.when(at == 0)
    def _():
        tally_ref[...] = jnp.zeros_like(tally_ref)

    tally_ref[...] += packed
    stats_ref[...] = jnp.broadcast_to(tally_ref[0:2, :][None], stats_ref.shape)


def forward(core, states, acts, w_hidden, w_head, members):
    rows, width = acts.shape
    half = width // 2
    tile = lambda cols: pl.BlockSpec((ROWS, cols), lambda i, core: (i, 0))
    return pl.pallas_call(
        forward_kernel,
        grid_spec=pltpu.PrefetchScalarGridSpec(
            num_scalar_prefetch=1,
            grid=(rows // ROWS,),
            in_specs=[
                pl.BlockSpec((ROWS // 8, width), lambda i, core: (i, 0)),
                tile(width),
                pl.BlockSpec(memory_space=pltpu.VMEM),
                pl.BlockSpec((1, width), lambda i, core: (0, 0)),
            ],
            out_specs=[
                pl.BlockSpec((width, ROWS), lambda i, core: (0, i)),
                tile(half),
                tile(half),
                tile(width),
                pl.BlockSpec((1, ROWS), lambda i, core: (0, i)),
                pl.BlockSpec((members, 2, 128), lambda i, core: (0, 0, 0)),
            ],
            scratch_shapes=[pltpu.VMEM((ROWS, width), BF16), pltpu.VMEM((8, 128), F32)],
        ),
        out_shape=[
            jax.ShapeDtypeStruct((width, rows), BF16),
            jax.ShapeDtypeStruct((rows, half), BF16),
            jax.ShapeDtypeStruct((rows, half), BF16),
            jax.ShapeDtypeStruct((rows, width), BF16),
            jax.ShapeDtypeStruct((1, rows), F32),
            jax.ShapeDtypeStruct((members, 2, 128), F32),
        ],
        compiler_params=pltpu.CompilerParams(vmem_limit_bytes=30 << 20),
        cost_estimate=pl.CostEstimate(flops=2 * rows * width * width, bytes_accessed=20 << 20, transcendentals=2 * rows * width),
        name="forward",
    )(core, states, acts, w_hidden, w_head)


def split(value):
    high = value.astype(BF16)
    return high, (value - high.astype(F32)).astype(BF16)


def middle_kernel(states_here, first_ref, stats_ref, here_ref, there_ref, target_ref, keep_ref, came_ref, h_ref, bo_ref, bp_ref, extra_ref, log_ref, grad_ref):
    rows, half = keep_ref.shape
    peaks = stats_ref[:, 0, :]
    peak = jnp.max(peaks, 0, keepdims=True)
    mass = jnp.sum(stats_ref[:, 1, :] * jnp.exp(peaks - peak), 0, keepdims=True)
    lane = lax.broadcasted_iota(jnp.int32, (1, 128), 1)
    log_partition = jnp.where(lane < states_here, peak + jnp.log(jnp.where(lane < states_here, mass, 1.0)), 0.0)
    log_ref[...] = log_partition
    at = lax.broadcasted_iota(jnp.int32, (8, 128), 0)
    pair = jnp.where(at == 0, log_partition, target_ref[...])
    state = lax.broadcasted_iota(jnp.int32, (128, rows), 0)
    row = lax.broadcasted_iota(jnp.int32, (128, rows), 1)
    spread = ((row >> 3) == state).astype(F32)
    pair = jnp.dot(pair, spread, precision=lax.Precision.HIGHEST, preferred_element_type=F32)
    log_rows, target_rows = pair[0:1], pair[1:2]
    lead = (lax.broadcasted_iota(jnp.int32, (1, rows), 1) & 7) == 0

    def graded(score, flag):
        is_data = jnp.logical_and(lead, jnp.broadcast_to(flag, lead.shape) == 1)
        gap = score - target_rows
        grad = penalty_weight * jnp.exp(score - log_rows)
        grad = grad + jnp.where(is_data, gap - penalty_weight, 0.0)
        loss = jnp.where(is_data, penalty_weight * (log_rows - score) + 0.5 * gap * gap, 0.0)
        return grad, loss

    grad_here, loss = graded(here_ref[...], first_ref[0])
    grad_there, _ = graded(there_ref[...], first_ref[1])
    at = lax.broadcasted_iota(jnp.int32, (8, rows), 0)
    grads = jnp.where(at == 0, grad_here, grad_there)
    grad_ref[...] = grads.T
    loss = jnp.sum(loss, 1, keepdims=True)

    def scaled(i, carry):
        r = pl.ds(pl.multiple_of(i * 64, 64), 64)
        bo_ref[r, :] = (keep_ref[r, :].astype(F32) * grad_ref[r, 0:1]).astype(BF16)
        bp_ref[r, :] = (came_ref[r, :].astype(F32) * grad_ref[r, 1:2]).astype(BF16)
        return carry

    lax.fori_loop(0, rows // 64, scaled, 0)
    high, low = split(grad_here)
    weights = jnp.where(at == 0, high.astype(F32), low.astype(F32))
    weights = jnp.where(at < 2, weights, 0.0).astype(BF16)
    head = jnp.dot(weights, h_ref[...], preferred_element_type=F32)
    head = head[0:1] + head[1:2]
    loss = jnp.broadcast_to(loss, (1, half // 2))
    parts = [head[:, i * (half // 2) : (i + 1) * (half // 2)] for i in range(4)] + [loss]
    pack_extra(extra_ref, parts)


def pack_extra(ref, parts):
    at = lax.broadcasted_iota(jnp.int32, ref.shape, 0)
    out = jnp.zeros(ref.shape, F32)
    for i, part in enumerate(parts):
        high, low = split(part)
        out = jnp.where(at == i, high.astype(F32), out)
        out = jnp.where(at == i + 8, low.astype(F32), out)
    ref[...] = out.astype(BF16)


def middle(first, stats, here, there, targets, keep, came, h, states_here):
    rows, half = keep.shape
    whole = pl.BlockSpec(memory_space=pltpu.VMEM)
    return pl.pallas_call(
        functools.partial(middle_kernel, states_here),
        in_specs=[pl.BlockSpec(memory_space=pltpu.SMEM)] + [whole] * 7,
        out_specs=[whole] * 4,
        out_shape=[
            jax.ShapeDtypeStruct((rows, half), BF16),
            jax.ShapeDtypeStruct((rows, half), BF16),
            jax.ShapeDtypeStruct((16, half // 2), BF16),
            jax.ShapeDtypeStruct((1, 128), F32),
        ],
        scratch_shapes=[pltpu.VMEM((rows, 8), F32)],
        compiler_params=pltpu.CompilerParams(vmem_limit_bytes=8 << 20),
        cost_estimate=pl.CostEstimate(flops=1 << 30, bytes_accessed=9 << 20, transcendentals=0),
        name="middle",
    )(first, stats, here, there, targets, keep, came, h)


def gradient_kernel(spot_ref, xo_ref, xp_ref, bo_ref, bp_ref, extra_ref, ox_ref, oy_ref):
    depth = xo_ref.shape[-1]
    half = bo_ref.shape[1] // 2
    at_x = spot_ref[0]
    at_y = pl.multiple_of(spot_ref[1] * 16, 16)
    count = oy_ref.shape[0]

    def rows_x(ref):
        return ref[:, at_x, :, :].reshape(-1, depth)

    def rows_y(ref):
        return jnp.concatenate([ref[:, i, pl.ds(at_y, 16), :].reshape(-1, depth) for i in range(4)], 0)

    total = jnp.dot(rows_x(xo_ref), bo_ref[:, :half], preferred_element_type=F32)
    total += jnp.dot(rows_x(xp_ref), bp_ref[:, :half], preferred_element_type=F32)
    ox_ref[:count, :] = total.astype(BF16)
    ox_ref[count:, :] = extra_ref[...]
    total = jnp.dot(rows_y(xo_ref), bo_ref[:, half:], preferred_element_type=F32)
    total += jnp.dot(rows_y(xp_ref), bp_ref[:, half:], preferred_element_type=F32)
    oy_ref[...] = total.astype(BF16)


def gradient(spot, xo, xp, bo, bp, extra):
    depth = xo.shape[-1]
    half = bo.shape[1] // 2
    count = xo.shape[0] * xo.shape[2]
    whole = pl.BlockSpec(memory_space=pltpu.VMEM)
    return pl.pallas_call(
        gradient_kernel,
        in_specs=[pl.BlockSpec(memory_space=pltpu.SMEM)] + [whole] * 5,
        out_specs=[whole] * 2,
        out_shape=[jax.ShapeDtypeStruct((count + 16, half), BF16), jax.ShapeDtypeStruct((count, half), BF16)],
        compiler_params=pltpu.CompilerParams(vmem_limit_bytes=12 << 20),
        cost_estimate=pl.CostEstimate(flops=8 * count * half * depth, bytes_accessed=4 << 20, transcendentals=0),
        name="gradient",
    )(spot, xo, xp, bo, bp, extra)


def ordered_extra(scratch_ref, order_ref, values):
    for k, value in enumerate(values):
        scratch_ref[order_ref[k]] = value
    total = scratch_ref[0]
    for k in range(1, len(values)):
        total = total + scratch_ref[k]
    return total


def fold_kernel(lead, with_extra, spot_ref, *refs):
    own, got, outs = refs[0], refs[1:4], refs[4:8]
    rest = refs[8:]
    if lead:
        take = lambda ref, k: ref[pl.ds(pl.multiple_of(spot_ref[k] * 128, 128), 128), :].astype(F32)
    else:
        take = lambda ref, k: jnp.concatenate(
            [ref[pl.ds(pl.multiple_of(z * 64 + spot_ref[k] * 16, 16), 16), :] for z in range(8)], 0
        ).astype(F32)
    for k in (1, 2, 3, 0):
        value = take(own, k)
        for ref in got:
            value += take(ref, k)
        outs[k][:128, :] = value.astype(outs[k].dtype)
    if with_extra:
        whole = [ref[512:528, :].astype(F32) for ref in (own, *got)]
        total = ordered_extra(rest[0], spot_ref.at[pl.ds(4, 4)], [v[:8] + v[8:] for v in whole])
        high, low = split(total)
        block = jnp.concatenate([high.astype(F32), low.astype(F32)], 0)
        for k in range(4):
            outs[k][128:144, :] = block.astype(outs[k].dtype)


def fold(spot, own, got, lead, with_extra):
    whole = pl.BlockSpec(memory_space=pltpu.VMEM)
    height = 144 if with_extra else 128
    cols = own.shape[1]
    return pl.pallas_call(
        functools.partial(fold_kernel, lead, with_extra),
        in_specs=[pl.BlockSpec(memory_space=pltpu.SMEM)] + [whole] * 4,
        out_specs=[whole] * 4,
        out_shape=[jax.ShapeDtypeStruct((height, cols), F32 if k == 0 else BF16) for k in range(4)],
        scratch_shapes=[pltpu.VMEM((4, 8, cols), F32)] if with_extra else [],
        compiler_params=pltpu.CompilerParams(vmem_limit_bytes=6 << 20),
        cost_estimate=pl.CostEstimate(flops=1 << 20, bytes_accessed=3 << 20, transcendentals=0),
        name="fold",
    )(spot, own, *got)


def join_kernel(order_ref, *refs):
    ax, ay, out_ref, scratch_ref = refs[0:4], refs[4:8], refs[8], refs[9]
    half = ax[0].shape[1]
    whole = [ref[128:144, :].astype(F32) for ref in ax]
    total = ordered_extra(scratch_ref, order_ref, [v[:8] + v[8:] for v in whole])
    pieces = [total[i : i + 1, j * 128 : (j + 1) * 128] for i in range(5) for j in range(half // 128)]
    high, low = split(pieces[16])
    pieces[16:] = [high.astype(F32), low.astype(F32)]
    tail = []
    for k in range(3):
        at = lax.broadcasted_iota(jnp.int32, (8, 128), 0)
        block = jnp.zeros((8, 128), F32)
        for i, piece in enumerate(pieces[8 * k : 8 * k + 8]):
            block = jnp.where(at == i, piece, block)
        tail.append(block)
    tail = jnp.concatenate(tail, 1).astype(BF16)
    for z in range(8):
        for c in range(2):
            r = slice(z * 16 + c * 8, z * 16 + c * 8 + 8)
            sx = sum(ref[r, :].astype(F32) for ref in ax)
            sy = sum(ref[r, :].astype(F32) for ref in ay)
            out_ref[2 * z + c, :, :half] = sx.astype(BF16)
            out_ref[2 * z + c, :, half : 2 * half] = sy.astype(BF16)
            out_ref[2 * z + c, :, 2 * half :] = tail


def join(order, ax, ay):
    whole = pl.BlockSpec(memory_space=pltpu.VMEM)
    half = ax[0].shape[1]
    return pl.pallas_call(
        join_kernel,
        in_specs=[pl.BlockSpec(memory_space=pltpu.SMEM)] + [whole] * 8,
        out_specs=whole,
        out_shape=jax.ShapeDtypeStruct((16, 8, 2 * half + 384), BF16),
        scratch_shapes=[pltpu.VMEM((4, 8, half), F32)],
        compiler_params=pltpu.CompilerParams(vmem_limit_bytes=4 << 20),
        cost_estimate=pl.CostEstimate(flops=1 << 20, bytes_accessed=2 << 20, transcendentals=0),
        name="join",
    )(order, *ax, *ay)


def last_kernel(scale, all_ref, hidden_ref, head_ref, loss_ref):
    half = hidden_ref.shape[1] // 2
    for c in range(2):
        hidden_ref[:, c * half : (c + 1) * half] = sum(all_ref[2 * z + c, :, :half].astype(F32) for z in range(8))
    tail = sum(all_ref[i, :, half:].astype(F32) for i in range(16))
    head_ref[0:8, :] = tail[:, 0:128]
    head_ref[8:16, :] = tail[:, 128:256]
    loss_ref[...] = (tail[0:1, 256:384] + tail[1:2, 256:384]) * scale


def last(everything, states_total):
    whole = pl.BlockSpec(memory_space=pltpu.VMEM)
    width = 2 * (everything.shape[2] - 384)
    return pl.pallas_call(
        functools.partial(last_kernel, 1.0 / states_total),
        in_specs=[whole],
        out_specs=[whole] * 3,
        out_shape=[
            jax.ShapeDtypeStruct((8, width), F32),
            jax.ShapeDtypeStruct((16, 128), F32),
            jax.ShapeDtypeStruct((1, 128), F32),
        ],
        compiler_params=pltpu.CompilerParams(vmem_limit_bytes=4 << 20),
        name="last",
    )(everything)


def whole_states(state_features):
    own = jnp.broadcast_to(state_features, (16, *state_features.shape))
    mine = lax.all_to_all(own, ("x", "y"), split_axis=0, concat_axis=0, tiled=True)
    other = shifted(mine, "c", 1)
    c = lax.axis_index("c")
    both = jnp.stack([jnp.where(c == 0, mine, other), jnp.where(c == 0, other, mine)], 1)
    return jnp.moveaxis(both, 2, 0).reshape(state_features.shape[0], -1).astype(F32)


def step(state_features, action_features, targets, w_hidden, w_head):
    states_here, actions_here, width = action_features.shape
    states_total = states_here * lax.axis_size("z")
    rows = states_here * actions_here
    x, y, c = lax.axis_index("x"), lax.axis_index("y"), lax.axis_index("c")
    members = lax.axis_size(ACT)
    states = whole_states(state_features)
    core = jnp.full((1,), c, jnp.int32)
    xt, keep, send, h, score, stats = forward(core, states, action_features.reshape(rows, width), w_hidden, w_head[None], members)
    stats = lax.all_to_all(stats, ACT, split_axis=0, concat_axis=0, tiled=True)
    score_there = shifted(score, "c", 1)
    came = shifted(send, "c", 1)
    xt_there = shifted(xt, "c", 1)
    member = lax.axis_index(ACT)
    first = jnp.stack([member == 0, member + 1 - 2 * c == 0]).astype(jnp.int32)
    padded = jnp.pad(targets[None], ((0, 0), (0, 128 - states_here)))
    b_here, b_there, extra, log_row = middle(first, stats, score, score_there, padded, keep, came, h, states_here)

    xo = xt.reshape(8, 4, 64, rows)
    xp = xt_there.reshape(8, 4, 64, rows)

    def piece(k):
        spot = jnp.stack([lax.rem(x + k, 4), lax.rem(y + k, 4)]).astype(jnp.int32)
        return gradient(spot, xo, xp, b_here, b_there, extra)

    got_x, got_y = [], []
    for k in (2, 1, 3):
        out_x, out_y = piece(k)
        got_x.append(shifted(out_x, "x", k))
        got_y.append(shifted(out_y, "y", k))
    own_x, own_y = piece(0)

    spots = lambda at, far: jnp.stack([lax.rem(at + k, 4) for k in range(4)] + [lax.rem(far + k, 4) for k in (0, 2, 3, 1)]).astype(jnp.int32)
    fx = fold(spots(y, x), own_x, got_x, False, True)
    fy = fold(spots(x, y), own_y, got_y, True, False)
    more_x, more_y = [fx[0]], [fy[0]]
    for k in (1, 2, 3):
        more_x.append(shifted(fx[k], "y", k))
    for k in (1, 2, 3):
        more_y.append(shifted(fy[k], "x", k))
    order = jnp.stack([lax.rem(y + k, 4) for k in (0, 3, 2, 1)]).astype(jnp.int32)
    joined = join(order, more_x, more_y)
    everything = lax.all_to_all(joined, ("z", "c"), split_axis=0, concat_axis=0, tiled=True)
    hidden, head, loss = last(everything, states_total)
    return (hidden, head.reshape(-1), log_row[0, :states_here], loss[0, 0])


def solution(mesh):
    finer = Mesh(mesh.devices.reshape(mesh.shape["state"], 4, 4, 2), EVERY)
    placed = (P("z", ACT), P("z", ACT, None), P("z"), P(), P())
    return jax.shard_map(
        step,
        mesh=finer,
        in_specs=placed,
        out_specs=(P(EVERY, None), P(), P("z"), P()),
        check_vma=False,
    )
```

time: 325 us -> 157 us (0.48)
  waiting for transfers between devices: 186 us -> 38.8 us
  blocking collectives: 62.6 us -> 14.8 us
  Pallas kernels: 0 us -> 46 us
  matrix products: 27.4 us -> 0 us
  local copies, waits for them, and re-layouts: 5.41 us -> 22.8 us
  starting transfers between devices: 15.4 us -> 32.4 us
  between operations: 16 us -> 0.78 us
  other arithmetic: 11.1 us -> 0.63 us
    reduce_scatter x1 -> x0, waiting for transfers between devices: 173 us -> none  [body(): lax.psum_scatter(lax.dot_general(flat_rows, back_grad, (((0,), (0,)), (()...]
    pallas_call x0 -> x10, Pallas kernels: none -> 46 us  [the longest x4 18.6 us: gradient(): pl.pallas_call(gradient_kernel, in_specs=[pl.BlockSpec(memory_space=pltpu...]
    psum x4 -> x0, blocking collectives: 42.7 us -> none  [over_axes(): return functools.reduce(lax.psum, axes, value)]
    dot_general x2 -> x0, matrix products: 27.4 us -> none  [the longest x1 14 us: body(): lax.dot_general(flat_rows, back_grad, (((0,), (0,)), ((), ())), preferred...]
    ppermute x0 -> x16, waiting for transfers between devices: none -> 21.7 us  [shifted(): lax.ppermute(value, axis, [(i, (i + step) % count) for i in range(count)])]
    unnamed x8 -> x34, local copies, waits for them, and re-layouts: 0.02 us -> 20.1 us
    ppermute x0 -> x16, starting transfers between devices: none -> 14.1 us  [shifted(): lax.ppermute(value, axis, [(i, (i + step) % count) for i in range(count)])]
    reduce_sum x6 -> x0, other arithmetic: 9.83 us -> none  [the longest x1 4.57 us: body(): head_local = jnp.sum(grad_flat[:, None] * head_input, 0)]
  transfers between devices with their start and end apart: 4 -> 18, of which waited for: 3 -> 8; matrix products, arithmetic and copies ran while one was open for 2% -> 1% of each run, Pallas kernels for 0% -> 13%
where the time goes in v1:
time: 157 us; the launch traced here: 156 us
  Pallas kernels  46 us (29%)
  waiting for transfers between devices  38.8 us (25%)
  starting transfers between devices  32.4 us (21%)
  local copies, waits for them, and re-layouts  22.8 us (15%)
  blocking collectives  14.8 us (9%)
    ppermute x16, waiting for transfers between devices, shifted(): lax.ppermute(value, axis, [(i, (i + step) % count) for i in range(count)])  21.7 us
    unnamed x34, local copies, waits for them, and re-layouts  20.1 us
    pallas_call x4, Pallas kernels, gradient(): pl.pallas_call(gradient_kernel, in_specs=[pl.BlockSpec(memory_space=pltpu...  18.6 us
    pallas_call x1, Pallas kernels, forward(): pl.pallas_call(forward_kernel, grid_spec=pltpu.PrefetchScalarGridSpec(num...  18.1 us
    all_to_all x1, blocking collectives, whole_states(): lax.all_to_all(own, ('x', 'y'), split_axis=0, concat_axis=0, tiled=True)  14.8 us
    all_to_all x1, starting transfers between devices, step(): lax.all_to_all(joined, ('z', 'c'), split_axis=0, concat_axis=0, tiled=True)  14.2 us
    ppermute x16, starting transfers between devices, shifted(): lax.ppermute(value, axis, [(i, (i + step) % count) for i in range(count)])  14.1 us
    all_to_all x1, waiting for transfers between devices, step(): lax.all_to_all(joined, ('z', 'c'), split_axis=0, concat_axis=0, tiled=True)  13.2 us
  transfers between devices with their start and end apart: 18, of which 8 were waited for; matrix products, arithmetic and copies ran while one was open for 1% of the time, Pallas kernels for 13%

profile of v1, /device:TPU:1, one launch (start us, length us, event | category | flops | bytes accessed | tf_op | source)
XLA Modules:
  0.0 156.2 jit_solution(5908431528028875247)
XLA Ops:
  0.6 0.8 broadcast_in_dim.13
  1.4 14.8 %all_to_all.15 = bf16[16,96,64]{1,2,0:T(8,128)(2,1)S(1)} all-to-all(bf16[16,96,64]{1,2,0:T(8,128)(2,1)S(1)} %broadcast_in_dim.13), channel_id=1, replica_groups=mesh['z'=8,'x'=4,'y'=4,'c'=2] {'x','y'}, dimensions={0} | all-to-all | bytes 393216 | tf_op jit(solution)/shard_map/all_to_all | solution.py:374
  16.2 2.0 %collective-permute-start = (bf16[16,96,64]{1,2,0:T(8,128)(2,1)S(1)}, bf16[16,96,64]{1,2,0:T(8,128)(2,1)S(1)}, u32[]{:S(2)}, u32[]{:S(2)}) collective-permute-start(bf16[16,96,64]{1,2,0:T(8,128)(2,1)S(1)} %all_to_all.15), channel_id=1, source_target_pairs={{0,1},{1,0},{2,3},{3,2},{4,5},{5,4},{6,7},{7,6},{8,9},{9,8},{10,11... | collective-permute-start | bytes 589832 | tf_op jit(solution)/shard_map/ppermute | solution.py:26
  18.3 1.2 collective-permute-done
  19.5 0.1 maximum_convert_fusion
  19.6 1.2 copy.11.s_ref
  20.8 1.1 copy-done.10
  22.0 3.4 %copy-done.13 = bf16[2048,2048]{1,0:T(8,128)(2,1)S(1)} copy-done((bf16[2048,2048]{1,0:T(8,128)(2,1)S(1)}, bf16[2048,2048]{1,0:T(8,128)(2,1)}, u32[]{:S(2)}) %copy-start.13) | copy-done | bytes 8388632
  25.4 1.9 %copy-done.14 = bf16[96,8,2048]{2,1,0:T(8,128)(2,1)S(1)} copy-done((bf16[96,8,2048]{2,1,0:T(8,128)(2,1)S(1)}, bf16[96,8,2048]{2,1,0:T(8,128)(2,1)}, u32[]{:S(2)}) %copy-start.14) | copy-done | bytes 3145752
  27.2 18.1 %forward.1 = (bf16[2048,768]{1,0:T(8,128)(2,1)S(1)}, bf16[768,1024]{1,0:T(8,128)(2,1)S(1)}, bf16[768,1024]{1,0:T(8,128)(2,1)}, bf16[768,2048]{1,0:T(8,128)(2,1)S...) custom-call(s32[1]{0:T(128)} %bitcast.8.core_ref, f32[96,2048]{1,0:T(8,128)S(1)} %copy-done.10, ...), custom_call_target="tpu_custom_call" | custom-call | flops 6442450944 | bytes 20971520 | tf_op jit(solution)/shard_map/forward/pallas_call | solution.py:99
  45.3 1.7 %copy-done.6 = bf16[768,2048]{1,0:T(8,128)(2,1)} copy-done((bf16[768,2048]{1,0:T(8,128)(2,1)}, bf16[768,2048]{1,0:T(8,128)(2,1)S(1)}, u32[]{:S(2)}) %copy-start.6) | copy-done | bytes 3145752
  47.0 1.2 copy-done.8
  48.2 0.4 collective-permute-start.1
  48.6 0.1 collective-permute-start.3
  48.7 0.1 add_convert_fusion.first_ref
  48.8 4.1 %all-to-all-start.1 = ((f32[32,2,128]{2,1,0:T(2,128)}), f32[32,2,128]{2,1,0:T(2,128)S(1)}, u32[]{:S(2)}, u32[]{:S(2)}) async-start(f32[32,2,128]{2,1,0:T(2,128)} %get-tuple-element.34), calls=%async_computation.1 | async-start | bytes 65536 | tf_op jit(solution)/shard_map/all_to_all | solution.py:390
  52.9 0.3 collective-permute-start.2
  53.2 0.1 pad_add_fusion.4.spot_ref
  53.3 3.0 %collective-permute-done.2.there_ref = f32[1,768]{1,0:T(1,128)S(1)} collective-permute-done((f32[1,768]{1,0:T(1,128)S(1)}, f32[1,768]{1,0:T(1,128)S(1)}, u32[]{:S(2)}, u32[]{:S(2)}) %collective-permute-start.2) | collective-permute-done | bytes 3104 | tf_op jit(solution)/shard_map/ppermute | solution.py:26
  56.3 3.9 %all-to-all-done.1.stats_ref = f32[32,2,128]{2,1,0:T(2,128)S(1)} async-done(((f32[32,2,128]{2,1,0:T(2,128)}), f32[32,2,128]{2,1,0:T(2,128)S(1)}, u32[]{:S(2)}, u32[]{:S(2)}) %all-to-all-start.1) | async-done | bytes 32800 | tf_op jit(solution)/shard_map/all_to_all | solution.py:390
  60.1 0.0 collective-permute-done.3.came_ref
  60.1 1.9 %copy-done.7 = bf16[768,2048]{1,0:T(8,128)(2,1)S(1)} copy-done((bf16[768,2048]{1,0:T(8,128)(2,1)S(1)}, bf16[768,2048]{1,0:T(8,128)(2,1)}, u32[]{:S(2)}) %copy-start.7) | copy-done | bytes 3145752
  62.0 1.4 copy-done.9
  63.4 3.9 %middle.1 = (bf16[768,1024]{1,0:T(8,128)(2,1)S(1)}, bf16[768,1024]{1,0:T(8,128)(2,1)S(1)}, bf16[16,512]{1,0:T(8,128)(2,1)S(1)}, f32[1,128]{1,0:T(1,128)S(1)}) custom-call(s32[2]{0:T(128)S(1)} %add_convert_fusion.first_ref, f32[32,2,128]{2,1,0:T(2,128)S(1)} %all-to-all-done.1.stats_ref, f32[1,768]{1,0:T(1,128)S(1)} %get-tuple-element.35.here_ref, ...), custom_call_target="tpu_custom_call" | custom-call | flops 1073741824 | bytes 9437184 | tf_op jit(solution)/shard_map/middle/pallas_call | solution.py:201
  67.4 0.0 collective-permute-done.1
  67.4 5.7 %gradient.7 = (bf16[528,512]{1,0:T(8,128)(2,1)}, bf16[512,512]{1,0:T(8,128)(2,1)}) custom-call(s32[2]{0:T(128)S(1)} %pad_add_fusion.4.spot_ref, bf16[8,4,64,768]{3,2,1,0:T(8,128)(2,1)S(1)} %bitcast.28, bf16[8,4,64,768]{3,2,1,0:T(8,128)(2,1)} %bitcast.16.xp_ref, bf16[768,1024]{1,0:T(8,128)(2,1)S(1)} %get-tuple-element.39.bo_ref, ...), custom_call_target="tpu_custom_call" | custom-call | flops 1610612736 | bytes 4194304 | tf_op jit(solution)/shard_map/gradient/pallas_call | solution.py:245
  73.1 0.9 collective-permute-start.12
  74.0 0.1 pad_add_fusion.2.spot_ref
  74.1 0.1 pad_add_fusion.3.spot_ref
  74.2 1.4 copy-done.1
  75.6 1.4 copy-done.4
  77.0 4.6 %gradient.6 = (bf16[528,512]{1,0:T(8,128)(2,1)}, bf16[512,512]{1,0:T(8,128)(2,1)}) custom-call(s32[2]{0:T(128)S(1)} %pad_add_fusion.3.spot_ref, bf16[8,4,64,768]{3,2,1,0:T(8,128)(2,1)S(1)} %bitcast.29, bf16[8,4,64,768]{3,2,1,0:T(8,128)(2,1)} %bitcast.16.xp_ref, bf16[768,1024]{1,0:T(8,128)(2,1)S(1)} %copy-done.1, bf16[768,1024]{1,0:T(8,128)(2,1)S(1)} %copy-done.4, ...), custom_call_target="tpu_custom_call" | custom-call | flops 1610612736 | bytes 4194304 | tf_op jit(solution)/shard_map/gradient/pallas_call | solution.py:245
  81.6 0.6 collective-permute-start.11
  82.2 4.6 %gradient.5 = (bf16[528,512]{1,0:T(8,128)(2,1)}, bf16[512,512]{1,0:T(8,128)(2,1)}) custom-call(s32[2]{0:T(128)S(1)} %pad_add_fusion.2.spot_ref, bf16[8,4,64,768]{3,2,1,0:T(8,128)(2,1)S(1)} %bitcast.30, bf16[8,4,64,768]{3,2,1,0:T(8,128)(2,1)} %bitcast.16.xp_ref, bf16[768,1024]{1,0:T(8,128)(2,1)S(1)} %copy-done.1, bf16[768,1024]{1,0:T(8,128)(2,1)S(1)} %copy-done.4, ...), custom_call_target="tpu_custom_call" | custom-call | flops 1610612736 | bytes 4194304 | tf_op jit(solution)/shard_map/gradient/pallas_call | solution.py:245
  86.8 0.8 collective-permute-start.10
  87.6 0.9 collective-permute-start.6
  88.5 0.6 collective-permute-start.5
  89.1 0.0 collective-permute-done.12.refs_3_
  89.1 1.0 collective-permute-start.4
  90.0 0.1 stack.103.spot_ref
  90.1 0.1 pad_add_fusion.1.spot_ref
  90.2 1.4 copy-done.2
  91.6 1.4 copy-done.5
  93.0 3.7 %gradient.4 = (bf16[528,512]{1,0:T(8,128)(2,1)S(1)}, bf16[512,512]{1,0:T(8,128)(2,1)S(1)}) custom-call(s32[2]{0:T(128)S(1)} %pad_add_fusion.1.spot_ref, bf16[8,4,64,768]{3,2,1,0:T(8,128)(2,1)S(1)} %bitcast.31, bf16[8,4,64,768]{3,2,1,0:T(8,128)(2,1)} %bitcast.16.xp_ref, bf16[768,1024]{1,0:T(8,128)(2,1)S(1)} %copy-done.2, bf16[768,1024]{1,0:T(8,128)(2,1)S(1)} %copy-done.5, ...), custom_call_target="tpu_custom_call" | custom-call | flops 1610612736 | bytes 4194304 | tf_op jit(solution)/shard_map/gradient/pallas_call | solution.py:245
  96.7 0.8 copy-done.11
  97.5 9.6 %collective-permute-done.11.refs_2_ = bf16[512,512]{1,0:T(8,128)(2,1)} collective-permute-done((bf16[512,512]{1,0:T(8,128)(2,1)}, bf16[512,512]{1,0:T(8,128)(2,1)}, u32[]{:S(2)}, u32[]{:S(2)}) %collective-permute-start.11) | collective-permute-done | bytes 524320 | tf_op jit(solution)/shard_map/ppermute | solution.py:26
  107.2 1.6 %fold.3 = (f32[128,512]{1,0:T(8,128)S(1)}, bf16[128,512]{1,0:T(8,128)(2,1)S(1)}, bf16[128,512]{1,0:T(8,128)(2,1)S(1)}, bf16[128,512]{1,0:T(8,128)(2,1)S(1)}) custom-call(s32[8]{0:T(128)S(1)} %stack.103.spot_ref, bf16[512,512]{1,0:T(8,128)(2,1)S(1)} %get-tuple-element.50.refs_0_, bf16[512,512]{1,0:T(8,128)(2,1)} %collective-permute-done.10.refs_1_, ...), custom_call_target="tpu_custom_call" | custom-call | flops 1048576 | bytes 3145728 | tf_op jit(solution)/shard_map/fold/pallas_call | solution.py:292
  108.8 0.1 collective-permute-start.13
  108.9 0.1 stack.92.spot_ref
  109.0 3.9 %collective-permute-done.4.refs_1_ = bf16[528,512]{1,0:T(8,128)(2,1)} collective-permute-done((bf16[528,512]{1,0:T(8,128)(2,1)}, bf16[528,512]{1,0:T(8,128)(2,1)}, u32[]{:S(2)}, u32[]{:S(2)}) %collective-permute-start.4) | collective-permute-done | bytes 540704 | tf_op jit(solution)/shard_map/ppermute | solution.py:26
  112.8 1.0 copy-done.12
  113.9 1.7 %fold.2 = (f32[144,512]{1,0:T(8,128)S(1)}, bf16[144,512]{1,0:T(8,128)(2,1)S(1)}, bf16[144,512]{1,0:T(8,128)(2,1)S(1)}, bf16[144,512]{1,0:T(8,128)(2,1)S(1)}) custom-call(s32[8]{0:T(128)S(1)} %stack.92.spot_ref, bf16[528,512]{1,0:T(8,128)(2,1)S(1)} %copy-done.12, bf16[528,512]{1,0:T(8,128)(2,1)} %collective-permute-done.4.refs_1_, ...), custom_call_target="tpu_custom_call" | custom-call | flops 1048576 | bytes 3145728 | tf_op jit(solution)/shard_map/fold/pallas_call | solution.py:292
  115.6 1.3 collective-permute-start.7
  116.9 1.8 %collective-permute-start.8 = (bf16[144,512]{1,0:T(8,128)(2,1)S(1)}, bf16[144,512]{1,0:T(8,128)(2,1)S(1)}, u32[]{:S(2)}, u32[]{:S(2)}) collective-permute-start(bf16[144,512]{1,0:T(8,128)(2,1)S(1)} %get-tuple-element.48), channel_id=1, source_target_pairs={{0,4},{2,6},{4,0},{6,2},{1,5},{3,7},{5,1},{7,3},{8,12},{10,14},{12... | collective-permute-start | bytes 442376 | tf_op jit(solution)/shard_map/ppermute | solution.py:26
  118.7 1.2 collective-permute-start.9
  119.9 2.2 %collective-permute-start.14 = (bf16[128,512]{1,0:T(8,128)(2,1)S(1)}, bf16[128,512]{1,0:T(8,128)(2,1)S(1)}, u32[]{:S(2)}, u32[]{:S(2)}) collective-permute-start(bf16[128,512]{1,0:T(8,128)(2,1)S(1)} %get-tuple-element.56), channel_id=1, source_target_pairs={{0,16},{8,24},{16,0},{24,8},{1,17},{9,25},{17,1},{25,9},{2,18},{10... | collective-permute-start | bytes 393224 | tf_op jit(solution)/shard_map/ppermute | solution.py:26
  122.1 0.1 pad_add_fusion.order_ref
  122.1 3.1 %collective-permute-done.14.refs_6_ = bf16[128,512]{1,0:T(8,128)(2,1)S(1)} collective-permute-done((bf16[128,512]{1,0:T(8,128)(2,1)S(1)}, bf16[128,512]{1,0:T(8,128)(2,1)S(1)}, u32[]{:S(2)}, u32[]{:S(2)}) %collective-permute-start.14) | collective-permute-done | bytes 131104 | tf_op jit(solution)/shard_map/ppermute | solution.py:26
  125.2 0.9 collective-permute-done.15.refs_7_
  126.1 1.4 join.1
  127.6 14.2 %all-to-all-start.2 = ((bf16[16,8,1408]{2,1,0:T(8,128)(2,1)}), bf16[16,8,1408]{2,1,0:T(8,128)(2,1)S(1)}, u32[]{:S(2)}, u32[]{:S(2)}) async-start(bf16[16,8,1408]{2,1,0:T(8,128)(2,1)} %join.1), calls=%async_computation.2 | async-start | bytes 720896 | tf_op jit(solution)/shard_map/all_to_all | solution.py:423
  141.8 0.5 slice_bitcast_fusion
  142.3 13.2 %all-to-all-done.2.all_ref = bf16[16,8,1408]{2,1,0:T(8,128)(2,1)S(1)} async-done(((bf16[16,8,1408]{2,1,0:T(8,128)(2,1)}), bf16[16,8,1408]{2,1,0:T(8,128)(2,1)S(1)}, u32[]{:S(2)}, u32[]{:S(2)}) %all-to-all-start.2) | async-done | bytes 360480 | tf_op jit(solution)/shard_map/all_to_all | solution.py:423
  155.6 0.7 last.1
  (31 shorter events, 0.1 us)
Async XLA Ops:
  0.6 20.2 %copy-start.15 = (f32[2048]{0:T(1024)S(1)}, f32[2048]{0:T(1024)}, u32[]{:S(2)}) copy-start(f32[2048]{0:T(1024)} %param.9) | copy-start | bytes 24580
  16.2 3.2 %collective-permute-start = (bf16[16,96,64]{1,2,0:T(8,128)(2,1)S(1)}, bf16[16,96,64]{1,2,0:T(8,128)(2,1)S(1)}, u32[]{:S(2)}, u32[]{:S(2)}) collective-permute-start(bf16[16,96,64]{1,2,0:T(8,128)(2,1)S(1)} %all_to_all.15), channel_id=1, source_target_pairs={{0,1},{1,0},{2,3},{3,2},{4,5},{5,4},{6,7},{7,6},{8,9},{9,8},{10,11... | collective-permute-start | bytes 589832 | tf_op jit(solution)/shard_map/ppermute | solution.py:26
  20.8 1.1 copy-start.10
  22.0 3.4 %copy-start.13 = (bf16[2048,2048]{1,0:T(8,128)(2,1)S(1)}, bf16[2048,2048]{1,0:T(8,128)(2,1)}, u32[]{:S(2)}) copy-start(bf16[2048,2048]{1,0:T(8,128)(2,1)} %w_ref.1) | copy-start | bytes 25165828
  25.3 1.9 %copy-start.14 = (bf16[96,8,2048]{2,1,0:T(8,128)(2,1)S(1)}, bf16[96,8,2048]{2,1,0:T(8,128)(2,1)}, u32[]{:S(2)}) copy-start(bf16[96,8,2048]{2,1,0:T(8,128)(2,1)} %param.6) | copy-start | bytes 9437188
  27.2 26.0 %copy-start.16 = (f32[96]{0:T(128)S(1)}, f32[96]{0:T(128)}, u32[]{:S(2)}) copy-start(f32[96]{0:T(128)} %param.7) | copy-start | bytes 1156
  45.3 1.7 %copy-start.6 = (bf16[768,2048]{1,0:T(8,128)(2,1)}, bf16[768,2048]{1,0:T(8,128)(2,1)S(1)}, u32[]{:S(2)}) copy-start(bf16[768,2048]{1,0:T(8,128)(2,1)S(1)} %get-tuple-element.38.h_ref) | copy-start | bytes 9437188
  47.0 1.2 copy-start.8
  48.2 19.2 %collective-permute-start.1 = (bf16[2048,768]{1,0:T(8,128)(2,1)S(1)}, bf16[2048,768]{1,0:T(8,128)(2,1)}, u32[]{:S(2)}, u32[]{:S(2)}) collective-permute-start(bf16[2048,768]{1,0:T(8,128)(2,1)S(1)} %get-tuple-element.33), channel_id=1, source_target_pairs={{0,1},{1,0},{2,3},{3,2},{4,5},{5,4},{6,7},{7,6},{8,9},{9,8},{10,11... | collective-permute-start | bytes 9437192 | tf_op jit(solution)/shard_map/ppermute | solution.py:26
  48.6 11.5 %collective-permute-start.3 = (bf16[768,1024]{1,0:T(8,128)(2,1)}, bf16[768,1024]{1,0:T(8,128)(2,1)}, u32[]{:S(2)}, u32[]{:S(2)}) collective-permute-start(bf16[768,1024]{1,0:T(8,128)(2,1)} %get-tuple-element.37), channel_id=1, source_target_pairs={{0,1},{1,0},{2,3},{3,2},{4,5},{5,4},{6,7},{7,6},{8,9},{9,8},{10,11... | collective-permute-start | bytes 4718600 | tf_op jit(solution)/shard_map/ppermute | solution.py:26
  48.8 11.3 %all-to-all-start.1 = ((f32[32,2,128]{2,1,0:T(2,128)}), f32[32,2,128]{2,1,0:T(2,128)S(1)}, u32[]{:S(2)}, u32[]{:S(2)}) async-start(f32[32,2,128]{2,1,0:T(2,128)} %get-tuple-element.34), calls=%async_computation.1 | async-start | bytes 65536 | tf_op jit(solution)/shard_map/all_to_all | solution.py:390
  52.9 3.4 %collective-permute-start.2 = (f32[1,768]{1,0:T(1,128)S(1)}, f32[1,768]{1,0:T(1,128)S(1)}, u32[]{:S(2)}, u32[]{:S(2)}) collective-permute-start(f32[1,768]{1,0:T(1,128)S(1)} %get-tuple-element.35.here_ref), channel_id=1, source_target_pairs={{0,1},{1,0},{2,3},{3,2},{4,5},{5,4},{6,7},{7,6},{8,9},{9,8},{10,11... | collective-permute-start | bytes 9224 | tf_op jit(solution)/shard_map/ppermute | solution.py:26
  60.1 1.9 %copy-start.7 = (bf16[768,2048]{1,0:T(8,128)(2,1)S(1)}, bf16[768,2048]{1,0:T(8,128)(2,1)}, u32[]{:S(2)}) copy-start(bf16[768,2048]{1,0:T(8,128)(2,1)} %copy-done.6) | copy-start | bytes 9437188
  62.0 1.4 copy-start.9
  67.4 5.8 %copy-start = (bf16[768,1024]{1,0:T(8,128)(2,1)}, bf16[768,1024]{1,0:T(8,128)(2,1)S(1)}, u32[]{:S(2)}) copy-start(bf16[768,1024]{1,0:T(8,128)(2,1)S(1)} %get-tuple-element.39.bo_ref) | copy-start | bytes 4718596
  67.4 5.8 %copy-start.3 = (bf16[768,1024]{1,0:T(8,128)(2,1)}, bf16[768,1024]{1,0:T(8,128)(2,1)S(1)}, u32[]{:S(2)}) copy-start(bf16[768,1024]{1,0:T(8,128)(2,1)S(1)} %get-tuple-element.40.bp_ref) | copy-start | bytes 4718596
  73.1 15.9 %collective-permute-start.12 = (bf16[512,512]{1,0:T(8,128)(2,1)}, bf16[512,512]{1,0:T(8,128)(2,1)}, u32[]{:S(2)}, u32[]{:S(2)}) collective-permute-start(bf16[512,512]{1,0:T(8,128)(2,1)} %get-tuple-element.53), channel_id=1, source_target_pairs={{0,6},{2,0},{4,2},{6,4},{1,7},{3,1},{5,3},{7,5},{8,14},{10,8},{12,... | collective-permute-start | bytes 1572872 | tf_op jit(solution)/shard_map/ppermute | solution.py:26
  74.2 1.4 copy-start.1
  75.6 1.4 copy-start.4
  81.6 25.6 %collective-permute-start.11 = (bf16[512,512]{1,0:T(8,128)(2,1)}, bf16[512,512]{1,0:T(8,128)(2,1)}, u32[]{:S(2)}, u32[]{:S(2)}) collective-permute-start(bf16[512,512]{1,0:T(8,128)(2,1)} %get-tuple-element.52), channel_id=1, source_target_pairs={{0,2},{2,4},{4,6},{6,0},{1,3},{3,5},{5,7},{7,1},{8,10},{10,12},{12... | collective-permute-start | bytes 1572872 | tf_op jit(solution)/shard_map/ppermute | solution.py:26
  86.8 20.4 %collective-permute-start.10 = (bf16[512,512]{1,0:T(8,128)(2,1)}, bf16[512,512]{1,0:T(8,128)(2,1)}, u32[]{:S(2)}, u32[]{:S(2)}) collective-permute-start(bf16[512,512]{1,0:T(8,128)(2,1)} %get-tuple-element.51), channel_id=1, source_target_pairs={{0,4},{2,6},{4,0},{6,2},{1,5},{3,7},{5,1},{7,3},{8,12},{10,14},{12... | collective-permute-start | bytes 1572872 | tf_op jit(solution)/shard_map/ppermute | solution.py:26
  87.6 21.4 %collective-permute-start.6 = (bf16[528,512]{1,0:T(8,128)(2,1)}, bf16[528,512]{1,0:T(8,128)(2,1)}, u32[]{:S(2)}, u32[]{:S(2)}) collective-permute-start(bf16[528,512]{1,0:T(8,128)(2,1)} %get-tuple-element.45), channel_id=1, source_target_pairs={{0,24},{8,0},{16,8},{24,16},{1,25},{9,1},{17,9},{25,17},{2,26},{10... | collective-permute-start | bytes 1622024 | tf_op jit(solution)/shard_map/ppermute | solution.py:26
  88.5 20.5 %collective-permute-start.5 = (bf16[528,512]{1,0:T(8,128)(2,1)}, bf16[528,512]{1,0:T(8,128)(2,1)}, u32[]{:S(2)}, u32[]{:S(2)}) collective-permute-start(bf16[528,512]{1,0:T(8,128)(2,1)} %get-tuple-element.44), channel_id=1, source_target_pairs={{0,8},{8,16},{16,24},{24,0},{1,9},{9,17},{17,25},{25,1},{2,10},{10... | collective-permute-start | bytes 1622024 | tf_op jit(solution)/shard_map/ppermute | solution.py:26
  89.1 23.8 %collective-permute-start.4 = (bf16[528,512]{1,0:T(8,128)(2,1)}, bf16[528,512]{1,0:T(8,128)(2,1)}, u32[]{:S(2)}, u32[]{:S(2)}) collective-permute-start(bf16[528,512]{1,0:T(8,128)(2,1)} %get-tuple-element.43), channel_id=1, source_target_pairs={{0,16},{8,24},{16,0},{24,8},{1,17},{9,25},{17,1},{25,9},{2,18},{10... | collective-permute-start | bytes 1622024 | tf_op jit(solution)/shard_map/ppermute | solution.py:26
  90.2 1.4 copy-start.2
  91.6 1.4 copy-start.5
  96.7 0.8 copy-start.11
  108.8 13.3 %collective-permute-start.13 = (bf16[128,512]{1,0:T(8,128)(2,1)S(1)}, bf16[128,512]{1,0:T(8,128)(2,1)S(1)}, u32[]{:S(2)}, u32[]{:S(2)}) collective-permute-start(bf16[128,512]{1,0:T(8,128)(2,1)S(1)} %get-tuple-element.55), channel_id=1, source_target_pairs={{0,8},{8,16},{16,24},{24,0},{1,9},{9,17},{17,25},{25,1},{2,10},{10... | collective-permute-start | bytes 393224 | tf_op jit(solution)/shard_map/ppermute | solution.py:26
  112.8 1.0 copy-start.12
  115.6 10.5 %collective-permute-start.7 = (bf16[144,512]{1,0:T(8,128)(2,1)S(1)}, bf16[144,512]{1,0:T(8,128)(2,1)S(1)}, u32[]{:S(2)}, u32[]{:S(2)}) collective-permute-start(bf16[144,512]{1,0:T(8,128)(2,1)S(1)} %get-tuple-element.47), channel_id=1, source_target_pairs={{0,2},{2,4},{4,6},{6,0},{1,3},{3,5},{5,7},{7,1},{8,10},{10,12},{12... | collective-permute-start | bytes 442376 | tf_op jit(solution)/shard_map/ppermute | solution.py:26
  116.9 9.2 %collective-permute-start.8 = (bf16[144,512]{1,0:T(8,128)(2,1)S(1)}, bf16[144,512]{1,0:T(8,128)(2,1)S(1)}, u32[]{:S(2)}, u32[]{:S(2)}) collective-permute-start(bf16[144,512]{1,0:T(8,128)(2,1)S(1)} %get-tuple-element.48), channel_id=1, source_target_pairs={{0,4},{2,6},{4,0},{6,2},{1,5},{3,7},{5,1},{7,3},{8,12},{10,14},{12... | collective-permute-start | bytes 442376 | tf_op jit(solution)/shard_map/ppermute | solution.py:26
  118.7 7.4 %collective-permute-start.9 = (bf16[144,512]{1,0:T(8,128)(2,1)S(1)}, bf16[144,512]{1,0:T(8,128)(2,1)S(1)}, u32[]{:S(2)}, u32[]{:S(2)}) collective-permute-start(bf16[144,512]{1,0:T(8,128)(2,1)S(1)} %get-tuple-element.49), channel_id=1, source_target_pairs={{0,6},{2,0},{4,2},{6,4},{1,7},{3,1},{5,3},{7,5},{8,14},{10,8},{12,... | collective-permute-start | bytes 442376 | tf_op jit(solution)/shard_map/ppermute | solution.py:26
  119.9 5.3 %collective-permute-start.14 = (bf16[128,512]{1,0:T(8,128)(2,1)S(1)}, bf16[128,512]{1,0:T(8,128)(2,1)S(1)}, u32[]{:S(2)}, u32[]{:S(2)}) collective-permute-start(bf16[128,512]{1,0:T(8,128)(2,1)S(1)} %get-tuple-element.56), channel_id=1, source_target_pairs={{0,16},{8,24},{16,0},{24,8},{1,17},{9,25},{17,1},{25,9},{2,18},{10... | collective-permute-start | bytes 393224 | tf_op jit(solution)/shard_map/ppermute | solution.py:26
  122.0 4.1 %collective-permute-start.15 = (bf16[128,512]{1,0:T(8,128)(2,1)S(1)}, bf16[128,512]{1,0:T(8,128)(2,1)S(1)}, u32[]{:S(2)}, u32[]{:S(2)}) collective-permute-start(bf16[128,512]{1,0:T(8,128)(2,1)S(1)} %get-tuple-element.57), channel_id=1, source_target_pairs={{0,24},{8,0},{16,8},{24,16},{1,25},{9,1},{17,9},{25,17},{2,26},{10... | collective-permute-start | bytes 393224 | tf_op jit(solution)/shard_map/ppermute | solution.py:26
  127.6 28.0 %all-to-all-start.2 = ((bf16[16,8,1408]{2,1,0:T(8,128)(2,1)}), bf16[16,8,1408]{2,1,0:T(8,128)(2,1)S(1)}, u32[]{:S(2)}, u32[]{:S(2)}) async-start(bf16[16,8,1408]{2,1,0:T(8,128)(2,1)} %join.1), calls=%async_computation.2 | async-start | bytes 720896 | tf_op jit(solution)/shard_map/all_to_all | solution.py:423

commit v2 on v1

v2 whole, which is shorter than its diff:
```python
import functools

import jax
import jax.numpy as jnp
from jax import lax
from jax.experimental import pallas as pl
from jax.experimental.pallas import tpu as pltpu
from jax.sharding import Mesh
from jax.sharding import PartitionSpec as P

ACT = ("x", "y", "c")
EVERY = ("z", "x", "y", "c")
F32 = jnp.float32
BF16 = jnp.bfloat16

norm_epsilon = 1e-06
penalty_weight = 2.0


COLS = 256
EARLY = 2


def shifted(value, axis, step):
    count = lax.axis_size(axis)
    return lax.ppermute(value, axis, [(i, (i + step) % count) for i in range(count)])


def within(value, op):
    lane = lax.broadcasted_iota(jnp.int32, value.shape, 1)
    width = value.shape[1]
    for step in (1, 2, 4):
        low = pltpu.roll(value, step, 1)
        high = pltpu.roll(value, width - step, 1)
        value = op(value, jnp.where((lane & step) != 0, low, high))
    return value


def forward_kernel(height, ids_ref, mine_ref, other_ref, a_hbm, w_hbm, head_hbm, xt_ref, keep_ref, send_ref, h_ref, score_ref, stats_ref, s_ref, x_ref, a_ref, w_ref, head_ref, a_sems, w_sems, head_sem):
    rows, width = a_hbm.shape
    tiles = width // COLS
    core = ids_ref[2]
    spots = [pl.multiple_of(lax.rem(j + core * (tiles // 2), tiles) * COLS, COLS) for j in range(tiles)]
    a_copies, w_copies = [], []
    for i in range(rows // height):
        part = pl.ds(i * height, height)
        a_copies.append(pltpu.make_async_copy(a_hbm.at[part], a_ref.at[part], a_sems.at[i]))
    for j in range(tiles):
        part = pl.ds(j * COLS, COLS)
        w_copies.append(pltpu.make_async_copy(w_hbm.at[part], w_ref.at[part], w_sems.at[j]))
    head_copy = pltpu.make_async_copy(head_hbm, head_ref, head_sem)
    for copy in (*a_copies[:EARLY], *w_copies, *a_copies[EARLY:], head_copy):
        copy.start()
    lead = jnp.broadcast_to(core == 0, mine_ref.shape[1:])
    for i in range(mine_ref.shape[0]):
        mine, other = mine_ref[i].astype(F32), other_ref[i].astype(F32)
        pair = jnp.concatenate([jnp.where(lead, mine, other), jnp.where(lead, other, mine)], 0)
        s_ref[:, i * 128 : (i + 1) * 128] = pair.T

    def normalise(row):
        r = slice(row, row + 16)
        acts = a_ref[r, :].astype(F32)
        at = row // 8
        first = jnp.broadcast_to(s_ref[at : at + 1, :], (8, width))
        second = jnp.broadcast_to(s_ref[at + 1 : at + 2, :], (8, width))
        mixture = jnp.concatenate([first, second], 0) + acts
        scale = lax.rsqrt(jnp.mean(mixture * mixture, -1, keepdims=True) + norm_epsilon)
        x_ref[r, :] = (mixture * scale).astype(BF16)

    for i in range(EARLY):
        a_copies[i].wait()
        for row in range(i * height, (i + 1) * height, 16):
            normalise(row)
    for copy in (*w_copies, *a_copies[EARLY:], head_copy):
        copy.wait()
    tally = jnp.zeros((8, 128), F32)
    ahead = height // 16 // tiles
    for at in range(rows // height):
        r = slice(at * height, (at + 1) * height)
        total = jnp.zeros((height, 128), F32)
        for j in range(tiles):
            n = spots[j]
            x_cols = x_ref[r, pl.ds(n, COLS)]
            xt_ref[pl.ds(n, COLS), r] = x_cols.T
            preact = jnp.dot(x_ref[r, :], w_ref[:, pl.ds(n, COLS)], preferred_element_type=F32)
            if at + EARLY < rows // height:
                for i in range(ahead):
                    normalise((at + EARLY) * height + (j * ahead + i) * 16)
            g = jax.nn.sigmoid(preact)
            gated = preact * g
            h = x_cols.astype(F32) + gated
            head = head_ref[:, pl.ds(n, COLS)]
            h_ref[r, pl.ds(n, COLS)] = h.astype(BF16)
            u = (head * (g + gated * (1.0 - g))).astype(BF16)
            if j < tiles // 2:
                keep_ref[r, j * COLS : (j + 1) * COLS] = u
            else:
                send_ref[r, j * COLS - width // 2 : (j + 1) * COLS - width // 2] = u
            part = h * head
            for k in range(COLS // 128):
                total += part[:, k * 128 : (k + 1) * 128]
        score = jnp.sum(total.T, 0, keepdims=True)
        score_ref[:, r] = score
        score = jnp.broadcast_to(score, (8, height))
        peak = within(score, jnp.maximum)
        mass = within(jnp.exp(score - peak), jnp.add)
        pair = jnp.where(lax.broadcasted_iota(jnp.int32, score.shape, 0) == 0, peak, mass)
        row = lax.broadcasted_iota(jnp.int32, (height, 128), 0)
        lane = lax.broadcasted_iota(jnp.int32, (height, 128), 1)
        pick = (row == (lane - at * (height // 8)) * 8).astype(F32)
        tally = tally + jnp.dot(pair, pick, precision=lax.Precision.HIGHEST, preferred_element_type=F32)
    at = lax.broadcasted_iota(jnp.int32, (8, 128), 0)
    payload = tally
    for k in range(rows // 128):
        payload = jnp.where(at == k + 2, score_ref[:, k * 128 : (k + 1) * 128], payload)
    stats_ref[...] = jnp.broadcast_to(payload[None], stats_ref.shape)


def forward(ids, mine, other, acts, w_hidden, w_head, members, height=256):
    rows, width = acts.shape
    half = width // 2
    whole = pl.BlockSpec(memory_space=pltpu.VMEM)
    away = pl.BlockSpec(memory_space=pltpu.HBM)
    acts = pltpu.with_memory_space_constraint(acts, pltpu.HBM)
    w_hidden = pltpu.with_memory_space_constraint(w_hidden, pltpu.HBM)
    w_head = pltpu.with_memory_space_constraint(w_head, pltpu.HBM)
    return pl.pallas_call(
        functools.partial(forward_kernel, height),
        in_specs=[pl.BlockSpec(memory_space=pltpu.SMEM), whole, whole, away, away, away],
        out_specs=[whole] * 6,
        out_shape=[
            jax.ShapeDtypeStruct((width, rows), BF16),
            jax.ShapeDtypeStruct((rows, half), BF16),
            jax.ShapeDtypeStruct((rows, half), BF16),
            jax.ShapeDtypeStruct((rows, width), BF16),
            jax.ShapeDtypeStruct((1, rows), F32),
            jax.ShapeDtypeStruct((members, 8, 128), F32),
        ],
        scratch_shapes=[
            pltpu.VMEM((rows // 8, width), F32),
            pltpu.VMEM((rows, width), BF16),
            pltpu.VMEM((rows, width), BF16),
            pltpu.VMEM((width, width), BF16),
            pltpu.VMEM((1, width), F32),
            pltpu.SemaphoreType.DMA((rows // height,)),
            pltpu.SemaphoreType.DMA((width // COLS,)),
            pltpu.SemaphoreType.DMA,
        ],
        compiler_params=pltpu.CompilerParams(vmem_limit_bytes=24 << 20),
        cost_estimate=pl.CostEstimate(flops=2 * rows * width * width, bytes_accessed=20 << 20, transcendentals=2 * rows * width),
        name="forward",
    )(ids, mine, other, acts, w_hidden, w_head)


def split(value):
    high = value.astype(BF16)
    return high, (value - high.astype(F32)).astype(BF16)


def middle_kernel(states_here, ids_ref, stats_ref, here_ref, target_ref, keep_ref, came_ref, h_ref, bo_ref, bp_ref, extra_ref, log_ref, grad_ref):
    rows, half = keep_ref.shape
    peaks = stats_ref[:, 0, :]
    peak = jnp.max(peaks, 0, keepdims=True)
    mass = jnp.sum(stats_ref[:, 1, :] * jnp.exp(peaks - peak), 0, keepdims=True)
    lane = lax.broadcasted_iota(jnp.int32, (1, 128), 1)
    log_partition = jnp.where(lane < states_here, peak + jnp.log(jnp.where(lane < states_here, mass, 1.0)), 0.0)
    log_ref[...] = log_partition
    at = lax.broadcasted_iota(jnp.int32, (8, 128), 0)
    pair = jnp.where(at == 0, log_partition, 0.0)
    state = lax.broadcasted_iota(jnp.int32, (128, rows), 0)
    row = lax.broadcasted_iota(jnp.int32, (128, rows), 1)
    spread = ((row >> 3) == state).astype(F32)
    pair = jnp.dot(pair, spread, precision=lax.Precision.HIGHEST, preferred_element_type=F32)
    log_rows = pair[0:1]
    goals = jnp.broadcast_to(target_ref[...], (8, states_here))
    target_rows = jnp.dot(goals, spread[:states_here], precision=lax.Precision.HIGHEST, preferred_element_type=F32)[0:1]
    member = ids_ref[0] * 8 + ids_ref[1] * 2 + ids_ref[2]
    lead = (lax.broadcasted_iota(jnp.int32, (1, rows), 1) & 7) == 0

    def graded(score, flag):
        is_data = jnp.logical_and(lead, jnp.broadcast_to(flag, lead.shape))
        gap = score - target_rows
        grad = penalty_weight * jnp.exp(score - log_rows)
        grad = grad + jnp.where(is_data, gap - penalty_weight, 0.0)
        loss = jnp.where(is_data, penalty_weight * (log_rows - score) + 0.5 * gap * gap, 0.0)
        return grad, loss

    grad_here, loss = graded(here_ref[...], member == 0)
    partner = ids_ref[0] * 8 + ids_ref[1] * 2 + 1 - ids_ref[2]
    sent = stats_ref[partner]
    there = jnp.concatenate([sent[k + 2 : k + 3] for k in range(rows // 128)], 1)
    grad_there, _ = graded(there, member + 1 - 2 * ids_ref[2] == 0)
    at = lax.broadcasted_iota(jnp.int32, (8, rows), 0)
    grads = jnp.where(at == 0, grad_here, grad_there)
    grad_ref[...] = grads.T
    loss = jnp.sum(loss, 1, keepdims=True)

    def scaled(i, carry):
        r = pl.ds(pl.multiple_of(i * 64, 64), 64)
        bo_ref[r, :] = (keep_ref[r, :].astype(F32) * grad_ref[r, 0:1]).astype(BF16)
        bp_ref[r, :] = (came_ref[r, :].astype(F32) * grad_ref[r, 1:2]).astype(BF16)
        return carry

    lax.fori_loop(0, rows // 64, scaled, 0)
    high, low = split(grad_here)
    weights = jnp.where(at == 0, high.astype(F32), low.astype(F32))
    weights = jnp.where(at < 2, weights, 0.0).astype(BF16)
    head = jnp.dot(weights, h_ref[...], preferred_element_type=F32)
    head = head[0:1] + head[1:2]
    pack_extra(extra_ref, [head[:, :half], head[:, half:], jnp.broadcast_to(loss, (1, half))])


def pack_extra(ref, parts):
    at = lax.broadcasted_iota(jnp.int32, ref.shape, 0)
    out = jnp.zeros(ref.shape, F32)
    for i, part in enumerate(parts):
        high, low = split(part)
        out = jnp.where(at == i, high.astype(F32), out)
        out = jnp.where(at == i + 8, low.astype(F32), out)
    ref[...] = out.astype(BF16)


def middle(ids, stats, here, targets, keep, came, h, states_here):
    rows, half = keep.shape
    whole = pl.BlockSpec(memory_space=pltpu.VMEM)
    return pl.pallas_call(
        functools.partial(middle_kernel, states_here),
        in_specs=[pl.BlockSpec(memory_space=pltpu.SMEM)] + [whole] * 6,
        out_specs=[whole] * 4,
        out_shape=[
            jax.ShapeDtypeStruct((rows, half), BF16),
            jax.ShapeDtypeStruct((rows, half), BF16),
            jax.ShapeDtypeStruct((16, half), BF16),
            jax.ShapeDtypeStruct((1, 128), F32),
        ],
        scratch_shapes=[pltpu.VMEM((rows, 8), F32)],
        compiler_params=pltpu.CompilerParams(vmem_limit_bytes=6 << 20),
        cost_estimate=pl.CostEstimate(flops=1 << 30, bytes_accessed=9 << 20, transcendentals=0),
        name="middle",
    )(ids, stats, here, targets, keep, came, h)


def ways(ids_ref):
    x, y, core = ids_ref[0], ids_ref[1], ids_ref[2]
    return jnp.where(core == 0, x, y), jnp.where(core == 0, y, x), core


def gradient_kernel(turn, ids_ref, xo_ref, xp_ref, bo_ref, bp_ref, extra_ref, out_ref):
    near, _, core = ways(ids_ref)
    at = lax.rem(near + turn, 4)
    base = at * jnp.where(core == 0, 64, 16)
    stride = jnp.where(core == 0, 16, 64)
    count = out_ref.shape[0] - 16

    def rows(ref):
        starts = [pl.multiple_of(z * 256 + base + i * stride, 16) for z in range(8) for i in range(4)]
        return jnp.concatenate([ref[pl.ds(start, 16), :] for start in starts], 0)

    total = jnp.dot(rows(xo_ref), bo_ref[...], preferred_element_type=F32)
    total += jnp.dot(rows(xp_ref), bp_ref[...], preferred_element_type=F32)
    out_ref[:count, :] = total.astype(BF16)
    out_ref[count:, :] = extra_ref[...]


def gradient(turn, ids, xo, xp, bo, bp, extra):
    width, depth = xo.shape
    half = bo.shape[1]
    count = width // 4
    whole = pl.BlockSpec(memory_space=pltpu.VMEM)
    return pl.pallas_call(
        functools.partial(gradient_kernel, turn),
        in_specs=[pl.BlockSpec(memory_space=pltpu.SMEM)] + [whole] * 5,
        out_specs=whole,
        out_shape=jax.ShapeDtypeStruct((count + 16, half), BF16),
        compiler_params=pltpu.CompilerParams(vmem_limit_bytes=12 << 20),
        cost_estimate=pl.CostEstimate(flops=4 * count * half * depth, bytes_accessed=4 << 20, transcendentals=0),
        name="gradient",
    )(ids, xo, xp, bo, bp, extra)


def ordered_extra(scratch_ref, order, values):
    for k, value in enumerate(values):
        scratch_ref[order[k]] = value
    total = scratch_ref[0]
    for k in range(1, len(values)):
        total = total + scratch_ref[k]
    return total


def fold_kernel(ids_ref, *refs):
    own, got, outs, scratch_ref = refs[0], refs[1:4], refs[4:8], refs[8]
    near, far, _ = ways(ids_ref)
    for k in (1, 2, 3, 0):
        spot = lax.rem(far + k, 4) * 16
        for z in range(8):
            r = pl.ds(pl.multiple_of(z * 64 + spot, 16), 16)
            value = own[r, :].astype(F32)
            for ref in got:
                value += ref[r, :].astype(F32)
            outs[k][z * 16 : z * 16 + 16, :] = value.astype(outs[k].dtype)
    whole = [ref[512:528, :].astype(F32) for ref in (own, *got)]
    total = ordered_extra(scratch_ref, [lax.rem(near + k, 4) for k in (0, 2, 3, 1)], [v[:8] + v[8:] for v in whole])
    high, low = split(total)
    block = jnp.concatenate([high.astype(F32), low.astype(F32)], 0)
    for k in range(4):
        outs[k][128:144, :] = block.astype(outs[k].dtype)


def fold(ids, own, got):
    whole = pl.BlockSpec(memory_space=pltpu.VMEM)
    cols = own.shape[1]
    return pl.pallas_call(
        fold_kernel,
        in_specs=[pl.BlockSpec(memory_space=pltpu.SMEM)] + [whole] * 4,
        out_specs=[whole] * 4,
        out_shape=[jax.ShapeDtypeStruct((144, cols), F32 if k == 0 else BF16) for k in range(4)],
        scratch_shapes=[pltpu.VMEM((4, 8, cols), F32)],
        compiler_params=pltpu.CompilerParams(vmem_limit_bytes=6 << 20),
        cost_estimate=pl.CostEstimate(flops=1 << 20, bytes_accessed=3 << 20, transcendentals=0),
        name="fold",
    )(ids, own, *got)


def join_kernel(ids_ref, *refs):
    got, out_ref, scratch_ref = refs[0:4], refs[4], refs[5]
    half = got[0].shape[1]
    _, far, _ = ways(ids_ref)
    whole = [ref[128:144, :].astype(F32) for ref in got]
    total = ordered_extra(scratch_ref, [lax.rem(far + k, 4) for k in (0, 3, 2, 1)], [v[:8] + v[8:] for v in whole])
    pieces = [total[i : i + 1, j * 128 : (j + 1) * 128] for i in range(2) for j in range(half // 128)]
    pieces += [part.astype(F32) for part in split(total[2:3, :128])]
    tail = []
    for k in range(3):
        at = lax.broadcasted_iota(jnp.int32, (8, 128), 0)
        block = jnp.zeros((8, 128), F32)
        for i, piece in enumerate(pieces[8 * k : 8 * k + 8]):
            block = jnp.where(at == i, piece, block)
        tail.append(block)
    tail = jnp.concatenate(tail, 1).astype(BF16)
    for i in range(16):
        out_ref[i, :, :half] = sum(ref[i * 8 : i * 8 + 8, :].astype(F32) for ref in got).astype(BF16)
        out_ref[i, :, half:] = tail


def join(ids, got):
    whole = pl.BlockSpec(memory_space=pltpu.VMEM)
    half = got[0].shape[1]
    return pl.pallas_call(
        join_kernel,
        in_specs=[pl.BlockSpec(memory_space=pltpu.SMEM)] + [whole] * 4,
        out_specs=whole,
        out_shape=jax.ShapeDtypeStruct((16, 8, half + 384), BF16),
        scratch_shapes=[pltpu.VMEM((4, 8, half), F32)],
        compiler_params=pltpu.CompilerParams(vmem_limit_bytes=4 << 20),
        cost_estimate=pl.CostEstimate(flops=1 << 20, bytes_accessed=2 << 20, transcendentals=0),
        name="join",
    )(ids, *got)


def last_kernel(scale, all_ref, hidden_ref, head_ref, loss_ref):
    half = hidden_ref.shape[1] // 2
    for c in range(2):
        hidden_ref[:, c * half : (c + 1) * half] = sum(all_ref[2 * z + c, :, :half].astype(F32) for z in range(8))
    tail = sum(all_ref[i, :, half:].astype(F32) for i in range(16))
    head_ref[0:8, :] = tail[:, 0:128]
    head_ref[8:16, :] = tail[:, 128:256]
    loss_ref[...] = (tail[0:1, 256:384] + tail[1:2, 256:384]) * scale


def last(everything, states_total):
    whole = pl.BlockSpec(memory_space=pltpu.VMEM)
    width = 2 * (everything.shape[2] - 384)
    return pl.pallas_call(
        functools.partial(last_kernel, 1.0 / states_total),
        in_specs=[whole],
        out_specs=[whole] * 3,
        out_shape=[
            jax.ShapeDtypeStruct((8, width), F32),
            jax.ShapeDtypeStruct((16, 128), F32),
            jax.ShapeDtypeStruct((1, 128), F32),
        ],
        compiler_params=pltpu.CompilerParams(vmem_limit_bytes=4 << 20),
        name="last",
    )(everything)


def gathered(state_features, ids):
    own = jnp.where(jnp.sum(ids) < 0, jnp.zeros_like(state_features), state_features)
    own = jnp.broadcast_to(own.T, (16, *state_features.shape[::-1]))
    mine = lax.all_to_all(own, ("x", "y"), split_axis=0, concat_axis=0, tiled=True)
    return mine, shifted(mine, "c", 1)


def step(state_features, action_features, targets, w_hidden, w_head):
    states_here, actions_here, width = action_features.shape
    states_total = states_here * lax.axis_size("z")
    rows = states_here * actions_here
    ids = jnp.stack([lax.axis_index(axis) for axis in (*ACT, "z")]).astype(jnp.int32)
    members = lax.axis_size(ACT)
    mine, other = gathered(state_features, ids)
    xt, keep, send, h, score, stats = forward(
        ids, mine, other, action_features.reshape(rows, width), w_hidden, w_head[None], members
    )
    stats = lax.all_to_all(stats, ACT, split_axis=0, concat_axis=0, tiled=True)
    came = shifted(send, "c", 1)
    xt_there = shifted(xt, "c", 1)
    b_here, b_there, extra, log_row = middle(ids, stats, score, targets[None], keep, came, h, states_here)

    def piece(k):
        return gradient(k, ids, xt, xt_there, b_here, b_there, extra)

    def turned(value, k, swap):
        pairs = []
        for i in range(32):
            px, py, pc = i // 8, i // 2 % 4, i % 2
            along_x = (pc == 0) != swap
            to = (px + k) % 4 * 8 + py * 2 + pc if along_x else px * 8 + (py + k) % 4 * 2 + pc
            pairs.append((i, to))
        return lax.ppermute(value, ACT, pairs)

    got = []
    for k in (2, 1, 3):
        out = piece(k)
        got.append(turned(out, k, False))
    folded = fold(ids, piece(0), got)
    more = [folded[0]]
    for k in (1, 2, 3):
        more.append(turned(folded[k], k, True))
    joined = join(ids, more)
    everything = lax.all_to_all(joined, ("z", "c"), split_axis=0, concat_axis=0, tiled=True)
    hidden, head, loss = last(everything, states_total)
    return (hidden, head.reshape(-1), log_row[0, :states_here], loss[0, 0])


def solution(mesh):
    finer = Mesh(mesh.devices.reshape(mesh.shape["state"], 4, 4, 2), EVERY)
    placed = (P("z", ACT), P("z", ACT, None), P("z"), P(), P())
    return jax.shard_map(
        step,
        mesh=finer,
        in_specs=placed,
        out_specs=(P(EVERY, None), P(), P("z"), P()),
        check_vma=False,
    )
```

time: 157 us -> 119 us (0.76)
  local copies, waits for them, and re-layouts: 22.8 us -> 0.56 us
  Pallas kernels: 46 us -> 30.9 us
  starting transfers between devices: 32.4 us -> 19.9 us
  blocking collectives: 14.8 us -> 26.4 us
    ppermute x0 -> x6, waiting for transfers between devices: none -> 24.9 us  [turned(): return lax.ppermute(value, ACT, pairs)]
    ppermute x16 -> x3, waiting for transfers between devices: 21.7 us -> 1.09 us  [shifted(): lax.ppermute(value, axis, [(i, (i + step) % count) for i in range(count)])]
    unnamed x34 -> x2, local copies, waits for them, and re-layouts: 20.1 us -> 0.01 us
    pallas_call x7 -> x6, Pallas kernels: 40 us -> 25.7 us  [the longest x1 15.2 us: forward(): pl.pallas_call(functools.partial(forward_kernel, height), in_specs=[pl.Bl...]
    all_to_all x1 -> x2, blocking collectives: 14.8 us -> 26.4 us  [the longest x1 14.8 us: gathered(): lax.all_to_all(own, ('x', 'y'), split_axis=0, concat_axis=0, tiled=True)]
    ppermute x16 -> x3, starting transfers between devices: 14.1 us -> 2.62 us  [shifted(): lax.ppermute(value, axis, [(i, (i + step) % count) for i in range(count)])]
    ppermute x0 -> x6, starting transfers between devices: none -> 6.48 us  [turned(): return lax.ppermute(value, ACT, pairs)]
    all_to_all x1 -> x0, starting transfers between devices: 4.05 us -> none  [step(): stats = lax.all_to_all(stats, ACT, split_axis=0, concat_axis=0, tiled=True)]
  transfers between devices with their start and end apart: 18 -> 10, of which waited for: 8 -> 6; matrix products, arithmetic and copies ran while one was open for 1% -> 0% of each run, Pallas kernels for 13% -> 9%
where the time goes in v2:
time: 119 us; the launch traced here: 118 us
  waiting for transfers between devices  39.2 us (33%)
  Pallas kernels  30.9 us (26%)
  blocking collectives  26.4 us (22%)
  starting transfers between devices  19.9 us (17%)
    ppermute x6, waiting for transfers between devices, turned(): return lax.ppermute(value, ACT, pairs)  24.9 us
    pallas_call x1, Pallas kernels, forward(): pl.pallas_call(functools.partial(forward_kernel, height), in_specs=[pl.Bl...  15.2 us
    all_to_all x1, blocking collectives, gathered(): lax.all_to_all(own, ('x', 'y'), split_axis=0, concat_axis=0, tiled=True)  14.8 us
    all_to_all x1, waiting for transfers between devices, step(): lax.all_to_all(joined, ('z', 'c'), split_axis=0, concat_axis=0, tiled=True)  13.2 us
    all_to_all x1, blocking collectives, step(): stats = lax.all_to_all(stats, ACT, split_axis=0, concat_axis=0, tiled=True)  11.6 us
    all_to_all x1, starting transfers between devices, step(): lax.all_to_all(joined, ('z', 'c'), split_axis=0, concat_axis=0, tiled=True)  10.8 us
    pallas_call x4, Pallas kernels, gradient(): pl.pallas_call(functools.partial(gradient_kernel, turn), in_specs=[pl.Blo...  9.38 us
    ppermute x6, starting transfers between devices, turned(): return lax.ppermute(value, ACT, pairs)  6.48 us
  transfers between devices with their start and end apart: 10, of which 6 were waited for; matrix products, arithmetic and copies ran while one was open for 0% of the time, Pallas kernels for 9%

profile of v2, /device:TPU:1, one launch (start us, length us, event | category | flops | bytes accessed | tf_op | source)
XLA Modules:
  0.0 118.5 jit_solution(2822800109860708562)
XLA Ops:
  0.6 0.7 select_bitcast_fusion
  1.4 14.8 %all_to_all.15.mine_ref = bf16[16,64,96]{2,1,0:T(8,128)(2,1)S(1)} all-to-all(bf16[16,64,96]{2,1,0:T(8,128)(2,1)S(1)} %broadcast_in_dim.13), channel_id=1, replica_groups=mesh['z'=8,'x'=4,'y'=4,'c'=2] {'x','y'}, dimensions={0} | all-to-all | bytes 393216 | tf_op jit(solution)/shard_map/all_to_all | solution.py:390
  16.2 2.0 %collective-permute-start = (bf16[16,64,96]{2,1,0:T(8,128)(2,1)S(1)}, bf16[16,64,96]{2,1,0:T(8,128)(2,1)S(1)}, u32[]{:S(2)}, u32[]{:S(2)}) collective-permute-start(bf16[16,64,96]{2,1,0:T(8,128)(2,1)S(1)} %all_to_all.15.mine_ref), channel_id=1, source_target_pairs={{0,1},{1,0},{2,3},{3,2},{4,5},{5,4},{6,7},{7,6},{8,9},{9,8},{10,11... | collective-permute-start | bytes 589832 | tf_op jit(solution)/shard_map/ppermute | solution.py:26
  18.3 0.1 pad_add_fusion.ids_ref
  18.3 1.1 collective-permute-done.other_ref
  19.4 0.0 copy-start
  19.4 15.2 %forward.1 = (bf16[2048,768]{1,0:T(8,128)(2,1)S(1)}, bf16[768,1024]{1,0:T(8,128)(2,1)S(1)}, bf16[768,1024]{1,0:T(8,128)(2,1)S(1)}, bf16[768,2048]{1,0:T(8,128)(2...) custom-call(s32[4]{0:T(128)S(1)} %pad_add_fusion.ids_ref, bf16[16,64,96]{2,1,0:T(8,128)(2,1)S(1)} %all_to_all.15.mine_ref, ...), custom_call_target="tpu_custom_call" | custom-call | flops 6442450944 | bytes 20971520 | tf_op jit(solution)/shard_map/forward/pallas_call | solution.py:127
  34.6 0.5 collective-permute-start.1
  35.1 0.1 collective-permute-start.2
  35.2 11.6 %all_to_all.16.stats_ref = f32[32,8,128]{2,1,0:T(8,128)S(1)} all-to-all(f32[32,8,128]{2,1,0:T(8,128)S(1)} %get-tuple-element.22), channel_id=1, replica_groups=mesh['z'=8,'x'=4,'y'=4,'c'=2] {'x','y','c'}, dimensions={0} | all-to-all | bytes 262144 | tf_op jit(solution)/shard_map/all_to_all | solution.py:404
  46.8 0.0 collective-permute-done.2.came_ref
  46.8 0.0 copy-done
  46.8 3.1 %middle.1 = (bf16[768,1024]{1,0:T(8,128)(2,1)S(1)}, bf16[768,1024]{1,0:T(8,128)(2,1)S(1)}, bf16[16,1024]{1,0:T(8,128)(2,1)S(1)}, f32[1,128]{1,0:T(1,128)S(1)}) custom-call(s32[4]{0:T(128)S(1)} %pad_add_fusion.ids_ref, f32[32,8,128]{2,1,0:T(8,128)S(1)} %all_to_all.16.stats_ref, f32[1,768]{1,0:T(1,128)S(1)} %get-tuple-element.23.here_ref, ...), custom_call_target="tpu_custom_call" | custom-call | flops 1073741824 | bytes 9437184 | tf_op jit(solution)/shard_map/middle/pallas_call | solution.py:226
  49.9 0.0 collective-permute-done.1.xp_ref
  49.9 2.4 %gradient.5 = bf16[528,1024]{1,0:T(8,128)(2,1)S(1)} custom-call(s32[4]{0:T(128)S(1)} %pad_add_fusion.ids_ref, bf16[2048,768]{1,0:T(8,128)(2,1)S(1)} %get-tuple-element.21.xo_ref, bf16[2048,768]{1,0:T(8,128)(2,1)S(1)} %collective-permute-done.1.xp_ref, bf16[768,1024]{1,0:T(8,128)(2,1)S(1)} %get-tuple-element.27.bo_ref, ...), custom_call_target="tpu_custom_call" | custom-call | flops 1610612736 | bytes 4194304 | tf_op jit(solution)/shard_map/gradient/pallas_call | solution.py:270
  52.3 0.8 collective-permute-start.3
  53.1 2.3 %gradient.6 = bf16[528,1024]{1,0:T(8,128)(2,1)S(1)} custom-call(s32[4]{0:T(128)S(1)} %pad_add_fusion.ids_ref, bf16[2048,768]{1,0:T(8,128)(2,1)S(1)} %get-tuple-element.21.xo_ref, bf16[2048,768]{1,0:T(8,128)(2,1)S(1)} %collective-permute-done.1.xp_ref, bf16[768,1024]{1,0:T(8,128)(2,1)S(1)} %get-tuple-element.27.bo_ref, ...), custom_call_target="tpu_custom_call" | custom-call | flops 1610612736 | bytes 4194304 | tf_op jit(solution)/shard_map/gradient/pallas_call | solution.py:270
  55.4 0.9 collective-permute-start.4
  56.3 2.3 %gradient.7 = bf16[528,1024]{1,0:T(8,128)(2,1)S(1)} custom-call(s32[4]{0:T(128)S(1)} %pad_add_fusion.ids_ref, bf16[2048,768]{1,0:T(8,128)(2,1)S(1)} %get-tuple-element.21.xo_ref, bf16[2048,768]{1,0:T(8,128)(2,1)S(1)} %collective-permute-done.1.xp_ref, bf16[768,1024]{1,0:T(8,128)(2,1)S(1)} %get-tuple-element.27.bo_ref, ...), custom_call_target="tpu_custom_call" | custom-call | flops 1610612736 | bytes 4194304 | tf_op jit(solution)/shard_map/gradient/pallas_call | solution.py:270
  58.6 2.0 %collective-permute-start.5 = (bf16[528,1024]{1,0:T(8,128)(2,1)S(1)}, bf16[528,1024]{1,0:T(8,128)(2,1)S(1)}, u32[]{:S(2)}, u32[]{:S(2)}) collective-permute-start(bf16[528,1024]{1,0:T(8,128)(2,1)S(1)} %gradient.7), channel_id=1, source_target_pairs={{0,24},{1,7},{2,26},{3,1},{4,28},{5,3},{6,30},{7,5},{8,0},{9,15},{... | collective-permute-start | bytes 3244040 | tf_op jit(solution)/shard_map/ppermute | solution.py:419
  60.6 2.4 %gradient.4.refs_0_ = bf16[528,1024]{1,0:T(8,128)(2,1)S(1)} custom-call(s32[4]{0:T(128)S(1)} %pad_add_fusion.ids_ref, bf16[2048,768]{1,0:T(8,128)(2,1)S(1)} %get-tuple-element.21.xo_ref, bf16[2048,768]{1,0:T(8,128)(2,1)S(1)} %collective-permute-done.1.xp_ref, bf16[768,1024]{1,0:T(8,128)(2,1)S(1)} %get-tuple-element.27.bo_ref, ...), custom_call_target="tpu_custom_call" | custom-call | flops 1610612736 | bytes 4194304 | tf_op jit(solution)/shard_map/gradient/pallas_call | solution.py:270
  63.0 5.2 %collective-permute-done.3.refs_1_ = bf16[528,1024]{1,0:T(8,128)(2,1)S(1)} collective-permute-done((bf16[528,1024]{1,0:T(8,128)(2,1)S(1)}, bf16[528,1024]{1,0:T(8,128)(2,1)S(1)}, u32[]{:S(2)}, u32[]{:S(2)}) %collective-permute-start.3) | collective-permute-done | bytes 1081376 | tf_op jit(solution)/shard_map/ppermute | solution.py:419
  68.2 11.5 %collective-permute-done.4.refs_2_ = bf16[528,1024]{1,0:T(8,128)(2,1)S(1)} collective-permute-done((bf16[528,1024]{1,0:T(8,128)(2,1)S(1)}, bf16[528,1024]{1,0:T(8,128)(2,1)S(1)}, u32[]{:S(2)}, u32[]{:S(2)}) %collective-permute-start.4) | collective-permute-done | bytes 1081376 | tf_op jit(solution)/shard_map/ppermute | solution.py:419
  79.8 0.0 collective-permute-done.5.refs_3_
  79.8 1.1 fold.1
  80.9 0.1 collective-permute-start.6
  81.0 2.0 %collective-permute-start.7 = (bf16[144,1024]{1,0:T(8,128)(2,1)S(1)}, bf16[144,1024]{1,0:T(8,128)(2,1)S(1)}, u32[]{:S(2)}, u32[]{:S(2)}) collective-permute-start(bf16[144,1024]{1,0:T(8,128)(2,1)S(1)} %get-tuple-element.32), channel_id=1, source_target_pairs={{0,4},{1,17},{2,6},{3,19},{4,0},{5,21},{6,2},{7,23},{8,12},{9,25},... | collective-permute-start | bytes 884744 | tf_op jit(solution)/shard_map/ppermute | solution.py:419
  83.0 0.8 collective-permute-start.8
  83.7 7.5 %collective-permute-done.6.refs_1_ = bf16[144,1024]{1,0:T(8,128)(2,1)S(1)} collective-permute-done((bf16[144,1024]{1,0:T(8,128)(2,1)S(1)}, bf16[144,1024]{1,0:T(8,128)(2,1)S(1)}, u32[]{:S(2)}, u32[]{:S(2)}) %collective-permute-start.6) | collective-permute-done | bytes 294944 | tf_op jit(solution)/shard_map/ppermute | solution.py:419
  91.2 0.0 collective-permute-done.7.refs_2_
  91.2 0.6 collective-permute-done.8.refs_3_
  91.8 1.4 %join.1 = bf16[16,8,1408]{2,1,0:T(8,128)(2,1)} custom-call(s32[4]{0:T(128)S(1)} %pad_add_fusion.ids_ref, f32[144,1024]{1,0:T(8,128)S(1)} %get-tuple-element.30.refs_0_, bf16[144,1024]{1,0:T(8,128)(2,1)S(1)} %collective-permute-done.6.refs_1_, bf16[144,1024]{1,0:T(8,128)(2,1)S(1)} %collective-permute-done.7.refs_2_, ...), custom_call_target="tpu_custom_call" | custom-call | flops 1048576 | bytes 2097152 | tf_op jit(solution)/shard_map/join/pallas_call | solution.py:348
  93.2 10.8 %all-to-all-start.2 = ((bf16[16,8,1408]{2,1,0:T(8,128)(2,1)}), bf16[16,8,1408]{2,1,0:T(8,128)(2,1)S(1)}, u32[]{:S(2)}, u32[]{:S(2)}) async-start(bf16[16,8,1408]{2,1,0:T(8,128)(2,1)} %join.1), calls=%async_computation.2 | async-start | bytes 720896 | tf_op jit(solution)/shard_map/all_to_all | solution.py:430
  104.1 0.5 slice_bitcast_fusion
  104.6 13.2 %all-to-all-done.2.all_ref = bf16[16,8,1408]{2,1,0:T(8,128)(2,1)S(1)} async-done(((bf16[16,8,1408]{2,1,0:T(8,128)(2,1)}), bf16[16,8,1408]{2,1,0:T(8,128)(2,1)S(1)}, u32[]{:S(2)}, u32[]{:S(2)}) %all-to-all-start.2) | async-done | bytes 360480 | tf_op jit(solution)/shard_map/all_to_all | solution.py:430
  117.8 0.7 last.1
  (1 shorter events, 0.0 us)
Async XLA Ops:
  16.2 3.2 %collective-permute-start = (bf16[16,64,96]{2,1,0:T(8,128)(2,1)S(1)}, bf16[16,64,96]{2,1,0:T(8,128)(2,1)S(1)}, u32[]{:S(2)}, u32[]{:S(2)}) collective-permute-start(bf16[16,64,96]{2,1,0:T(8,128)(2,1)S(1)} %all_to_all.15.mine_ref), channel_id=1, source_target_pairs={{0,1},{1,0},{2,3},{3,2},{4,5},{5,4},{6,7},{7,6},{8,9},{9,8},{10,11... | collective-permute-start | bytes 589832 | tf_op jit(solution)/shard_map/ppermute | solution.py:26
  19.4 27.4 %copy-start = (f32[96]{0:T(128)S(1)}, f32[96]{0:T(128)}, u32[]{:S(2)}) copy-start(f32[96]{0:T(128)} %param.7) | copy-start | bytes 1156
  34.6 15.3 %collective-permute-start.1 = (bf16[2048,768]{1,0:T(8,128)(2,1)S(1)}, bf16[2048,768]{1,0:T(8,128)(2,1)S(1)}, u32[]{:S(2)}, u32[]{:S(2)}) collective-permute-start(bf16[2048,768]{1,0:T(8,128)(2,1)S(1)} %get-tuple-element.21.xo_ref), channel_id=1, source_target_pairs={{0,1},{1,0},{2,3},{3,2},{4,5},{5,4},{6,7},{7,6},{8,9},{9,8},{10,11... | collective-permute-start | bytes 9437192 | tf_op jit(solution)/shard_map/ppermute | solution.py:26
  35.1 11.7 %collective-permute-start.2 = (bf16[768,1024]{1,0:T(8,128)(2,1)S(1)}, bf16[768,1024]{1,0:T(8,128)(2,1)S(1)}, u32[]{:S(2)}, u32[]{:S(2)}) collective-permute-start(bf16[768,1024]{1,0:T(8,128)(2,1)S(1)} %get-tuple-element.25), channel_id=1, source_target_pairs={{0,1},{1,0},{2,3},{3,2},{4,5},{5,4},{6,7},{7,6},{8,9},{9,8},{10,11... | collective-permute-start | bytes 4718600 | tf_op jit(solution)/shard_map/ppermute | solution.py:26
  52.3 15.9 %collective-permute-start.3 = (bf16[528,1024]{1,0:T(8,128)(2,1)S(1)}, bf16[528,1024]{1,0:T(8,128)(2,1)S(1)}, u32[]{:S(2)}, u32[]{:S(2)}) collective-permute-start(bf16[528,1024]{1,0:T(8,128)(2,1)S(1)} %gradient.5), channel_id=1, source_target_pairs={{0,16},{1,5},{2,18},{3,7},{4,20},{5,1},{6,22},{7,3},{8,24},{9,13},... | collective-permute-start | bytes 3244040 | tf_op jit(solution)/shard_map/ppermute | solution.py:419
  55.4 24.4 %collective-permute-start.4 = (bf16[528,1024]{1,0:T(8,128)(2,1)S(1)}, bf16[528,1024]{1,0:T(8,128)(2,1)S(1)}, u32[]{:S(2)}, u32[]{:S(2)}) collective-permute-start(bf16[528,1024]{1,0:T(8,128)(2,1)S(1)} %gradient.6), channel_id=1, source_target_pairs={{0,8},{1,3},{2,10},{3,5},{4,12},{5,7},{6,14},{7,1},{8,16},{9,11},{... | collective-permute-start | bytes 3244040 | tf_op jit(solution)/shard_map/ppermute | solution.py:419
  58.6 21.1 %collective-permute-start.5 = (bf16[528,1024]{1,0:T(8,128)(2,1)S(1)}, bf16[528,1024]{1,0:T(8,128)(2,1)S(1)}, u32[]{:S(2)}, u32[]{:S(2)}) collective-permute-start(bf16[528,1024]{1,0:T(8,128)(2,1)S(1)} %gradient.7), channel_id=1, source_target_pairs={{0,24},{1,7},{2,26},{3,1},{4,28},{5,3},{6,30},{7,5},{8,0},{9,15},{... | collective-permute-start | bytes 3244040 | tf_op jit(solution)/shard_map/ppermute | solution.py:419
  80.9 10.3 %collective-permute-start.6 = (bf16[144,1024]{1,0:T(8,128)(2,1)S(1)}, bf16[144,1024]{1,0:T(8,128)(2,1)S(1)}, u32[]{:S(2)}, u32[]{:S(2)}) collective-permute-start(bf16[144,1024]{1,0:T(8,128)(2,1)S(1)} %get-tuple-element.31), channel_id=1, source_target_pairs={{0,2},{1,9},{2,4},{3,11},{4,6},{5,13},{6,0},{7,15},{8,10},{9,17},{... | collective-permute-start | bytes 884744 | tf_op jit(solution)/shard_map/ppermute | solution.py:419
  81.0 10.2 %collective-permute-start.7 = (bf16[144,1024]{1,0:T(8,128)(2,1)S(1)}, bf16[144,1024]{1,0:T(8,128)(2,1)S(1)}, u32[]{:S(2)}, u32[]{:S(2)}) collective-permute-start(bf16[144,1024]{1,0:T(8,128)(2,1)S(1)} %get-tuple-element.32), channel_id=1, source_target_pairs={{0,4},{1,17},{2,6},{3,19},{4,0},{5,21},{6,2},{7,23},{8,12},{9,25},... | collective-permute-start | bytes 884744 | tf_op jit(solution)/shard_map/ppermute | solution.py:419
  83.0 8.9 %collective-permute-start.8 = (bf16[144,1024]{1,0:T(8,128)(2,1)S(1)}, bf16[144,1024]{1,0:T(8,128)(2,1)S(1)}, u32[]{:S(2)}, u32[]{:S(2)}) collective-permute-start(bf16[144,1024]{1,0:T(8,128)(2,1)S(1)} %get-tuple-element.33), channel_id=1, source_target_pairs={{0,6},{1,25},{2,0},{3,27},{4,2},{5,29},{6,4},{7,31},{8,14},{9,1},{... | collective-permute-start | bytes 884744 | tf_op jit(solution)/shard_map/ppermute | solution.py:419
  93.2 24.6 %all-to-all-start.2 = ((bf16[16,8,1408]{2,1,0:T(8,128)(2,1)}), bf16[16,8,1408]{2,1,0:T(8,128)(2,1)S(1)}, u32[]{:S(2)}, u32[]{:S(2)}) async-start(bf16[16,8,1408]{2,1,0:T(8,128)(2,1)} %join.1), calls=%async_computation.2 | async-start | bytes 720896 | tf_op jit(solution)/shard_map/all_to_all | solution.py:430
